TPU v7x, 128 devices: a whole 4x4x4 slice. The times are simulated.
128 devices in a mesh: blk: 64 (over x, y_hi, z, core), rep: 2 (over y_lo).
Axes of the slice: x: 4, y: 4 (y_hi: 2, y_lo: 2; y = y_hi * 2 + y_lo), z: 4, core: 2. Of those that a mesh axis runs over, the one named last changes fastest.
Arguments:
- captions: bfloat16 [24576, 768], P(('blk', 'rep')), may hold values from -512 to 512
- images: bfloat16 [24576, 768], P(('blk', 'rep')), may hold values from -512 to 512
- positives: int32 [24576], P(('blk', 'rep')), may hold values from 0 to 24575, each once
- valid: int32 [24576], P(('blk', 'rep')), may hold values from 0 to 1, as said below
Outputs:
- caption_loss: float32 [24576], P(('blk', 'rep'))
- image_loss: float32 [24576], P(('blk', 'rep'))
- loss: float32 [], replicated
Inputs may be any that keep to these rules, and one draw needn't show every extreme that they name: `positives`: each image row is the positive of exactly one caption; a program may pack several of these indices into one sent element. `valid`: the last image row is always real; a program may pack several of these flags into one sent element.
All inputs are finite; a program needn't handle non-finite values.
Results may differ from a plain program's by a relative error of at most 0.0003.
Values may be sent and summed in bfloat16 or wider, within the bound.
A program may use at most 128 MiB of HBM per device.

v0:
```python
import functools

import jax
import jax.numpy as jnp
from jax import lax
from jax.sharding import Mesh
from jax.sharding import PartitionSpec as P

BLK = ("blk_0", "blk_1", "blk_2", "blk_3")
BLK_REP = ("blk_0", "blk_1", "blk_2", "blk_3", "rep")


very_low = -1e30


def sent_to_all(shard, axis):
    count = lax.axis_size(axis)
    return lax.all_to_all(
        jnp.broadcast_to(shard[None], (count, *shard.shape)), axis, 0, 0, tiled=True
    )


def in_order(pieces, dim):
    dims = list(pieces.shape[1:])
    dims[dim] *= pieces.shape[0]
    return jnp.moveaxis(pieces, 0, dim).reshape(dims)


def gather_directly(shard, axis, dim):
    pieces = sent_to_all(shard, axis)
    return in_order(pieces, dim)


def all_in_one(shard, axis):
    leaves = jax.tree.leaves(shard)
    order = sorted(range(len(leaves)), key=lambda k: -leaves[k].size)
    width = (1, *leaves[order[0]].shape)[-1]
    lines = [
        jnp.pad(leaves[k].reshape(-1), (0, -leaves[k].size % width)).reshape(-1, width)
        for k in order
    ]
    both, at, found = (lax.all_gather(jnp.concatenate(lines), axis), 0, {})
    for k, line in zip(order, lines):
        piece = both[:, at : at + len(line)].reshape(len(both), -1)
        found[k] = piece[:, : leaves[k].size].reshape(-1, *leaves[k].shape)
        at += len(line)
    numbers = iter(range(len(leaves)))
    return jax.tree.map(lambda _: found[next(numbers)], shard)


def combined_by_axis(shard, axes, combine):
    for axis in axes:
        pieces = all_in_one(shard, axis)
        shard = jax.tree.map(lambda part: part[0], pieces)
        for k in range(1, lax.axis_size(axis)):
            shard = combine(shard, jax.tree.map(lambda part: part[k], pieces))
    return shard


def gathered_once(shard, axis):
    leaves = jax.tree.leaves(shard)
    order = sorted(range(len(leaves)), key=lambda k: -leaves[k].size)
    width = (1, *leaves[order[0]].shape)[-1]
    lines = [
        jnp.pad(leaves[k].reshape(-1), (0, -leaves[k].size % width)).reshape(-1, width)
        for k in order
    ]
    both, at, found = (sent_to_all(jnp.concatenate(lines), axis), 0, {})
    for k, line in zip(order, lines):
        piece = both[:, at : at + len(line)].reshape(len(both), -1)
        found[k] = piece[:, : leaves[k].size].reshape(-1, *leaves[k].shape)
        at += len(line)
    numbers = iter(range(len(leaves)))
    return jax.tree.map(lambda _: found[next(numbers)], shard)


def folded_in_pairs(pieces, combine):
    while len(jax.tree.leaves(pieces)[0]) > 1:
        pieces = jax.vmap(combine)(
            *(jax.tree.map(lambda part: part[side::2], pieces) for side in (0, 1))
        )
    return jax.tree.map(lambda part: part[0], pieces)


def joined_all(shard, axis, combine):
    pieces = gathered_once(shard, axis)
    return folded_in_pairs(pieces, combine)


def by_axis(shard, axes):
    return functools.reduce(lax.psum, axes, shard)


def fold_rows(running, scores, image_ok, is_positive):
    row_peak, row_total, row_match = running
    usable = image_ok[None, :] > 0
    highest = jnp.max(jnp.where(usable, scores, very_low), axis=1)
    renewed = jnp.maximum(row_peak, highest)
    powers = jnp.where(usable, jnp.exp(scores - renewed[:, None]), 0.0)
    row_total = jnp.sum(powers, axis=1)
    row_match = jnp.sum(jnp.where(is_positive, scores, 0.0), axis=1)
    return (renewed, row_total, row_match)


def fold_columns(running, scores, caption_live, is_positive):
    column_peak, column_total, column_match = running
    highest = jnp.max(jnp.where(caption_live, scores, very_low), axis=0)
    renewed = jnp.maximum(column_peak, highest)
    powers = jnp.where(caption_live, jnp.exp(scores - renewed[None, :]), 0.0)
    column_total = jnp.sum(powers, axis=0)
    column_match = jnp.sum(jnp.where(is_positive, scores, 0.0), axis=0)
    return (renewed, column_total, column_match)


def join_parts(first, second):
    peak_first, total_first, match_first = first
    peak_second, total_second, match_second = second
    highest = jnp.maximum(peak_first, peak_second)
    merged_total = total_first * jnp.exp(peak_first - highest) + total_second * jnp.exp(
        peak_second - highest
    )
    return (highest, merged_total, match_first + match_second)


def empty_columns(length):
    return (
        jnp.full((length,), very_low, jnp.float32),
        jnp.zeros((length,), jnp.float32),
        jnp.zeros((length,), jnp.float32),
    )


def local(captions, images, positives, valid):
    row_count = captions.shape[0]
    cycle_index = lax.axis_index(BLK)
    pair_index = lax.axis_index("rep")
    image_flags = lax.all_gather(valid, BLK_REP, axis=0, tiled=True).astype(jnp.float32)
    caption_ok = jnp.take(image_flags, positives, axis=0)
    image_block = gather_directly(images, "rep", 0)
    block_rows = image_block.shape[0]
    own_ok = lax.dynamic_slice_in_dim(
        image_flags, cycle_index * block_rows + pair_index * row_count, row_count
    )
    all_targets = gather_directly(positives, BLK, 0)
    image_start = cycle_index * block_rows
    block_ok = lax.dynamic_slice_in_dim(image_flags, image_start, block_rows)
    image_ids = image_start + lax.iota(jnp.int32, block_rows)
    piece = lax.all_gather(captions, BLK, axis=0, tiled=True)
    column_parts = empty_columns(block_rows)
    piece_count = piece.shape[0]
    piece_ok = jnp.take(image_flags, all_targets, axis=0)
    scores = lax.dot_general(
        piece, image_block, (((1,), (1,)), ((), ())), preferred_element_type=jnp.float32
    )
    is_positive = all_targets[:, None] == image_ids[None, :]
    fresh = fold_rows(empty_columns(piece_count), scores, block_ok, is_positive)
    row_parts = tuple((part for part in fresh))
    column_parts = fold_columns(column_parts, scores, piece_ok[:, None] > 0, is_positive)
    row_parts, column_parts = (row_parts, tuple(column_parts))
    row_joined = combined_by_axis((row_parts[0], row_parts[1], row_parts[2]), BLK, join_parts)
    row_state = tuple(
        (
            lax.dynamic_slice_in_dim(column, cycle_index * row_count, row_count)
            for column in row_joined
        )
    )
    column_joined = joined_all(
        (column_parts[0], column_parts[1], column_parts[2]), "rep", join_parts
    )
    own_columns = tuple(
        (
            lax.dynamic_slice_in_dim(column, pair_index * row_count, row_count)
            for column in column_joined
        )
    )
    caption_loss = caption_ok * (row_state[0] + jnp.log(row_state[1]) - row_state[2])
    image_loss = own_ok * (own_columns[0] + jnp.log(own_columns[1]) - own_columns[2])
    totals = (by_axis(jnp.sum(caption_loss), BLK_REP), by_axis(jnp.sum(image_loss), BLK_REP))
    loss = (totals[0] + totals[1]) / (2.0 * jnp.sum(image_flags))
    return (caption_loss, image_loss, loss)


def solution(mesh):
    torus = Mesh(
        mesh.devices.reshape(4, 2, 4, 2, mesh.shape["rep"]),
        ("blk_0", "blk_1", "blk_2", "blk_3", "rep"),
    )
    return jax.shard_map(
        local,
        mesh=torus,
        in_specs=(P(BLK_REP, None), P(BLK_REP, None), P(BLK_REP), P(BLK_REP)),
        out_specs=(P(BLK_REP), P(BLK_REP), P()),
        check_vma=False,
    )
```

profile of v0, /device:TPU:1, one launch (start us, length us, event | category | flops | bytes accessed | tf_op | source)
XLA Modules:
  0.0 402.6 jit_solution(18059547002845052368)
XLA Ops:
  8.1 0.9 dynamic-update-slice
  9.0 0.6 copy-done.2
  9.7 0.5 all-gather.10.cloned.1.call-update
  10.2 1.3 broadcast_in_dim.85
  11.5 12.5 %all-to-all-start.1 = ((s32[64,1,192]{2,1,0:T(1,128)}), s32[64,1,192]{2,1,0:T(1,128)S(1)}, u32[]{:S(2)}, u32[]{:S(2)}) async-start(s32[64,1,192]{2,1,0:T(1,128)} %broadcast_in_dim.85), calls=%async_computation.1 | async-start | bytes 131072 | tf_op jit(solution)/shard_map/all_to_all | solution.py:18
  24.0 0.7 compare_select_fusion.3
  24.7 8.9 %all-to-all-done.1 = s32[64,1,192]{2,1,0:T(1,128)S(1)} async-done(((s32[64,1,192]{2,1,0:T(1,128)}), s32[64,1,192]{2,1,0:T(1,128)S(1)}, u32[]{:S(2)}, u32[]{:S(2)}) %all-to-all-start.1) | async-done | bytes 49184 | tf_op jit(solution)/shard_map/all_to_all | solution.py:18
  33.6 1.8 broadcast_in_dim.81
  35.4 3.5 all-to-all-start
  39.4 159.7 %all-reduce.3.cloned.1.call-done = s32[24576]{0:T(1024)} async-done(((s32[24576]{0:T(1024)}), s32[24576]{0:T(1024)}) %all-reduce.3.cloned.1.call-update) | async-done | bytes 98320
  199.0 0.9 convert_element_type.3
  199.9 1.4 gather_fusion
  201.4 68.0 %gather_fusion.1 = f32[12288]{0:T(1024)S(1)} fusion(f32[24576]{0:T(1024)S(1)} %convert_element_type.3, s32[12288]{0:T(1024)S(1)} %broadcast_clamp_fusion), kind=kCustom, calls=%fused_computation.1 | custom fusion | bytes 147456 | tf_op jit(solution)/shard_map/jit(_take)/gather | solution.py:151
  269.6 17.6 %select_reduce_fusion.3 = (f32[12288]{0:T(1024)S(1)}, f32[12288,384]{1,0:T(8,128)}) fusion(pred[384]{0:T(512)(128)(4,1)S(1)} %dynamic-slice_compare_fusion, bf16[12288,768]{1,0:T(8,128)(2,1)} %all-gather.10.cloned.1.call-done, bf16[384,768]{1,0:T(8,128)(2,1)S(1)} %bitcast.210), kind=kOutput, calls=%fused_computation.5 | convolution fusion | flops 7257182208 | bytes 38388096 | tf_op jit(solution)/shard_map/dot_general | solution.py:152
  287.3 9.8 %select_reduce_fusion.1 = (f32[384]{0:T(512)S(1)}, f32[12288]{0:T(1024)S(1)}) fusion(f32[12288,384]{1,0:T(8,128)} %get-tuple-element.31, pred[12288]{0:T(1024)(128)(4,1)S(1)} %select_compare_fusion, f32[12288]{0:T(1024)S(1)} %broadcast_maximum_fusion, pred[384]{0:T(512)(128)(4,1)S(1)} %dynamic-slice_compare_fusion), kind=kLoop, calls=%fused_computation.3 | loop fusion | flops 23580288 | bytes 18986880 | tf_op jit(solution)/shard_map/reduce_max | solution.py:107
  297.1 2.1 copy-done
  299.2 10.8 %fusion = (f32[384]{0:T(512)S(1)}, f32[12288]{0:T(1024)S(1)}, f32[384]{0:T(512)S(1)}) fusion(f32[12288,384]{1,0:T(8,128)S(1)} %copy-done, s32[384]{0:T(512)S(1)} %iota_add_fusion, s32[12288]{0:T(1024)S(1)} %eq.15, f32[384]{0:T(512)S(1)} %broadcast_maximum_fusion.1, pred[12288]{0:T(1024)(128)(4,1)S(1)} %select_compare_fusion), kind=kLoop, calls=%fused_computation.7 | loop fusion | flops 33017088 | bytes 18991104 | tf_op jit(solution)/shard_map/reduce_sum | solution.py:111
  310.1 11.1 %all-gather.4 = f32[4,3,12288]{2,1,0:T(4,128)S(1)} all-gather(f32[1,3,12288]{2,1,0:T(4,128)S(1)} %maximum_bitcast_fusion), channel_id=2, replica_groups=mesh['blk_0'=4,'blk_1'=2,'blk_2'=4,'blk_3'=2,'rep'=2] {'blk_0'}, dimensions={0}, use_global_device_ids=true | all-gather | bytes 737280 | tf_op jit(solution)/shard_map/all_gather | solution.py:42
  321.4 0.5 fusion.18
  322.1 6.7 %all-gather.5 = f32[2,3,12288]{2,1,0:T(4,128)S(1)} all-gather(f32[1,3,12288]{2,1,0:T(4,128)S(1)} %maximum_bitcast_fusion.1), channel_id=3, replica_groups=mesh['blk_0'=4,'blk_1'=2,'blk_2'=4,'blk_3'=2,'rep'=2] {'blk_1'}, dimensions={0}, use_global_device_ids=true | all-gather | bytes 442368 | tf_op jit(solution)/shard_map/all_gather | solution.py:42
  329.2 11.4 %all-gather.6 = f32[4,3,12288]{2,1,0:T(4,128)S(1)} all-gather(f32[1,3,12288]{2,1,0:T(4,128)S(1)} %maximum_bitcast_fusion.2), channel_id=4, replica_groups=mesh['blk_0'=4,'blk_1'=2,'blk_2'=4,'blk_3'=2,'rep'=2] {'blk_2'}, dimensions={0}, use_global_device_ids=true | all-gather | bytes 737280 | tf_op jit(solution)/shard_map/all_gather | solution.py:42
  340.7 0.5 fusion.4
  341.3 0.6 broadcast_in_dim.89
  341.9 3.2 all-to-all-start.2
  345.2 9.4 %all-gather.7 = f32[2,3,12288]{2,1,0:T(4,128)S(1)} all-gather(f32[1,3,12288]{2,1,0:T(4,128)S(1)} %maximum_bitcast_fusion.3), channel_id=5, replica_groups=mesh['blk_0'=4,'blk_1'=2,'blk_2'=4,'blk_3'=2,'rep'=2] {'blk_3'}, dimensions={0}, use_global_device_ids=true | all-gather | bytes 442368 | tf_op jit(solution)/shard_map/all_gather | solution.py:42
  355.1 1.4 fusion.50
  357.8 8.0 %psum.84 = f32[]{:T(128)} all-reduce(f32[]{:T(128)S(6)} %add.321), channel_id=1, replica_groups=mesh['blk_0'=4,'blk_1'=2,'blk_2'=4,'blk_3'=2,'rep'=2] {'blk_0'}, use_global_device_ids=true, to_apply=%region_7.8 | all-reduce | flops 1 | bytes 8 | tf_op jit(solution)/shard_map/psum | solution.py:91
  365.8 5.9 %psum.83 = f32[]{:T(128)} all-reduce(f32[]{:T(128)} %psum.84), channel_id=1, replica_groups=mesh['blk_0'=4,'blk_1'=2,'blk_2'=4,'blk_3'=2,'rep'=2] {'blk_1'}, use_global_device_ids=true, to_apply=%region_8.9 | all-reduce | flops 1 | bytes 8 | tf_op jit(solution)/shard_map/psum | solution.py:91
  371.7 6.6 %psum.82 = f32[]{:T(128)} all-reduce(f32[]{:T(128)} %psum.83), channel_id=1, replica_groups=mesh['blk_0'=4,'blk_1'=2,'blk_2'=4,'blk_3'=2,'rep'=2] {'blk_2'}, use_global_device_ids=true, to_apply=%region_9.10 | all-reduce | flops 1 | bytes 8 | tf_op jit(solution)/shard_map/psum | solution.py:91
  378.3 0.7 convert_reduce_fusion
  379.0 9.3 %psum.81 = f32[]{:T(128)} all-reduce(f32[]{:T(128)} %psum.82), channel_id=1, replica_groups=mesh['blk_0'=4,'blk_1'=2,'blk_2'=4,'blk_3'=2,'rep'=2] {'blk_3'}, use_global_device_ids=true, to_apply=%region_10.11 | all-reduce | flops 1 | bytes 8 | tf_op jit(solution)/shard_map/psum | solution.py:91
  389.0 4.4 %psum.80 = f32[]{:T(128)} all-reduce(f32[]{:T(128)} %psum.81), channel_id=1, replica_groups=mesh['blk_0'=4,'blk_1'=2,'blk_2'=4,'blk_3'=2,'rep'=2] {'rep'}, use_global_device_ids=true, to_apply=%region_11.12 | all-reduce | flops 1 | bytes 8 | tf_op jit(solution)/shard_map/psum | solution.py:91
  (43 shorter events, 2.3 us)
Async XLA Ops:
  8.0 191.0 %all-reduce.3.cloned.1.call-start = ((), (), s32[]{:S(2)}) async-start(), calls=%async_computation.4 | async-start | bytes 196608
  9.0 0.6 copy-start.2
  9.6 260.0 %all-gather.10.cloned.1.call-start = ((), (), s32[]{:S(2)}) async-start(), calls=%async_computation.3 | async-start | bytes 19169280 | tf_op jit(solution)/shard_map/all_gather | solution.py:148
  11.5 22.1 %all-to-all-start.1 = ((s32[64,1,192]{2,1,0:T(1,128)}), s32[64,1,192]{2,1,0:T(1,128)S(1)}, u32[]{:S(2)}, u32[]{:S(2)}) async-start(s32[64,1,192]{2,1,0:T(1,128)} %broadcast_in_dim.85), calls=%async_computation.1 | async-start | bytes 131072 | tf_op jit(solution)/shard_map/all_to_all | solution.py:18
  35.4 234.1 %all-to-all-start = ((bf16[2,192,768]{2,1,0:T(8,128)(2,1)}), bf16[2,192,768]{2,1,0:T(8,128)(2,1)S(1)}, u32[]{:S(2)}, u32[]{:S(2)}) async-start(bf16[2,192,768]{2,1,0:T(8,128)(2,1)} %broadcast_in_dim.81), calls=%async_computation | async-start | bytes 1179648 | tf_op jit(solution)/shard_map/all_to_all | solution.py:18
  287.2 12.0 %copy-start = (f32[12288,384]{1,0:T(8,128)S(1)}, f32[12288,384]{1,0:T(8,128)}, u32[]{:S(2)}) copy-start(f32[12288,384]{1,0:T(8,128)} %get-tuple-element.31) | copy-start | bytes 56623108
  287.2 67.9 %copy-start.3 = (s32[192]{0:T(256)S(1)}, s32[192]{0:T(256)}, u32[]{:S(2)}) copy-start(s32[192]{0:T(256)} %param.6) | copy-start | bytes 2308
  287.3 91.0 %copy-start.1 = (s32[24576]{0:T(1024)S(1)}, s32[24576]{0:T(1024)}, u32[]{:S(2)}) copy-start(s32[24576]{0:T(1024)} %all-reduce.3.cloned.1.call-done) | copy-start | bytes 294916
  341.9 13.0 %all-to-all-start.2 = ((f32[2,3,384]{2,1,0:T(4,128)}), f32[2,3,384]{2,1,0:T(4,128)S(1)}, u32[]{:S(2)}, u32[]{:S(2)}) async-start(f32[2,3,384]{2,1,0:T(4,128)} %broadcast_in_dim.89), calls=%async_computation.2 | async-start | bytes 24576 | tf_op jit(solution)/shard_map/all_to_all | solution.py:18
Sparse Core Ops, SparseCore 0:
  13.5 185.4 all-reduce.2
Sparse Core Ops, SparseCore 1:
  13.4 115.4 all-gather.9
where the time goes:
time: 403 us
  waiting for transfers between devices  169 us (42%)
  local copies, waits for them, and re-layouts  77.3 us (19%)
  blocking collectives  72.7 us (18%)
  other arithmetic  27 us (7%)
  between operations  19.6 us (5%)
  starting transfers between devices  19.3 us (5%)
  matrix products  17.6 us (4%)
    unnamed x3, waiting for transfers between devices  160 us
    gather x1, local copies, waits for them, and re-layouts, local(): piece_ok = jnp.take(image_flags, all_targets, axis=0)  68 us
    all_gather x4, blocking collectives, all_in_one(): both, at, found = (lax.all_gather(jnp.concatenate(lines), axis), 0, {})  38.5 us
    psum x5, blocking collectives, by_axis(): return functools.reduce(lax.psum, axes, shard)  34.2 us
    all_to_all x3, starting transfers between devices, sent_to_all(): lax.all_to_all(jnp.broadcast_to(shard[None], (count, *shard.shape)), axis...  19.2 us
    dot_general x1, matrix products, local(): lax.dot_general(piece, image_block, (((1,), (1,)), ((), ())), preferred_e...  17.6 us
    reduce_sum x1, other arithmetic, fold_columns(): column_match = jnp.sum(jnp.where(is_positive, scores, 0.0), axis=0)  10.8 us
    reduce_max x1, other arithmetic, fold_columns(): highest = jnp.max(jnp.where(caption_live, scores, very_low), axis=0)  9.78 us
  transfers between devices with their start and end apart: 5, of which 2 were waited for; matrix products, arithmetic and copies ran while one was open for 19% of the time, Pallas kernels for 0%

commit v1 on v0

v1 whole, which is shorter than its diff:
```python
import functools

import jax
import jax.numpy as jnp
from jax import lax
from jax.experimental import pallas as pl
from jax.experimental.pallas import tpu as pltpu
from jax.sharding import Mesh
from jax.sharding import PartitionSpec as P

AXES = ("blk_0", "blk_1", "blk_2", "blk_3", "rep")
MESH = pl.DeviceIdType.MESH

ROWS = 192
PIECE = 64
WIDTH = 768
TILE = 2 * ROWS
BLOCK = 256
TILES = 8
BLOCKS = 6
LOW = -1e30
LOG2E = 1.4426950408889634
LN2 = 0.6931471805599453

FROM_LEFT = ((3, 0, 0), (3, 0, 1), (3, 0, 2), (2, 0, 0), (2, 0, 1), (3, 1, 2), (2, 1, 1))
FROM_RIGHT = ((1, 0, 0), (1, 0, 1), (1, 0, 2), (1, 1, 0), (2, 0, 2), (1, 1, 1), (2, 1, 0))
FROM_SIDE = ((0, 1, 0), (0, 1, 1), (0, 1, 2), (3, 1, 0), (3, 1, 1), (1, 1, 2), (2, 1, 2))
ARRIVALS = (FROM_LEFT, FROM_RIGHT, FROM_SIDE)
ROUNDS = 7
SLOT = {(0, 0, t): t for t in range(3)}
for _link, _list in enumerate(ARRIVALS):
    for _r, _chunk in enumerate(_list):
        SLOT[_chunk] = 3 * (_r + 1) + _link


def sent(link, r):
    d, s, t = ARRIVALS[link][r]
    if link == 0:
        return SLOT[((d + 1) % 4, s, t)]
    if link == 1:
        return SLOT[((d + 3) % 4, s, t)]
    return SLOT[(d, 1 - s, t)]


def release(link, r):
    return max(sent(link, k) // 3 for k in range(r + 1))


def items():
    done, order, starts, pairs = set(), [], {}, {}
    ready = (1, 2, 3, 5, 6, 7)
    for r in range(1, ROUNDS + 1):
        blocks = [b for b in range(BLOCKS) if ready[b] <= r]
        new = [b for b in blocks if ready[b] == r]
        first = [(p, b) for b in new for p in range(r)]
        later = [(r, b) for b in blocks]
        fresh = [i for i in first + later if i not in done]
        starts[r] = len(order)
        pairs[r] = len(order) + len([i for i in first if i not in done])
        order += fresh
        done |= set(fresh)
    return order, starts, pairs


ORDER, STARTS, PAIRS_AT = items()
ITEMS = len(ORDER)


def segments():
    found = []
    for i, (p, b) in enumerate(ORDER):
        if found:
            k, p0, b0, dp, db, n = found[-1]
            if n == 1:
                step = (p - p0, b - b0)
                if step in ((0, 1), (1, 0)):
                    found[-1] = (k, p0, b0, *step, 2)
                    continue
            elif (p0 + dp * n, b0 + db * n) == (p, b):
                found[-1] = (k, p0, b0, dp, db, n + 1)
                continue
        found.append((i, p, b, 0, 0, 1))
    return found


SEGMENTS = segments()


def place(i):
    tile, block = jnp.int32(0), jnp.int32(0)
    for k, p0, b0, dp, db, _ in SEGMENTS:
        tile = jnp.where(i >= k, p0 + dp * (i - k), tile)
        block = jnp.where(i >= k, b0 + db * (i - k), block)
    return tile, block


def row_place(slot, core):
    return (slot // 3) * TILE + core * ROWS + (slot % 3) * PIECE


def kernel(
    cap_in, img_in, pos_in, valid_in,
    cap_out, img_out, loss_out,
    cap, img, score0, score1, key, row_max, row_sum, row_match,
    col_max, col_sum, col_match, col_bias, col_id,
    meta, table, own_ok, row_msg, row_got, col_msg, col_got, part, part_got, part2, part2_got,
    load_sem, cap_send, cap_recv, img_send, img_recv, core_send, core_recv,
    meta_send, meta_recv, table_send, table_recv, row_send, row_recv, col_send, col_recv,
    a_send, a_recv, b_send, b_recv,
):
    x, yh, z, c, yl = (lax.axis_index(a) for a in AXES)

    def group_a(d, s, o):
        return (lax.rem(x + d, 4), yh, z, lax.rem(c + o, 2), lax.rem(yl + s, 2))

    def group_b(d, s):
        return (x, lax.rem(yh + s, 2), lax.rem(z + d, 4), c, lax.rem(yl + s, 2))

    members_a = [(d, s, o) for d in range(4) for s in range(2) for o in range(2) if (d, s, o) != (0, 0, 0)]
    members_b = [(d, s) for d in range(4) for s in range(2) if (d, s) != (0, 0)]

    def copy(src, dst, ssem, rsem, target):
        return pltpu.make_async_remote_copy(
            src_ref=src, dst_ref=dst, send_sem=ssem, recv_sem=rsem, device_id=target, device_id_type=MESH
        )

    def place_a(d, s, o):
        return (d * 2 + s) * 2 + o

    def place_b(d, s):
        return d * 2 + s

    load_cap = pltpu.make_async_copy(cap_in, cap.at[pl.ds(0, ROWS)], load_sem.at[0])
    load_img = pltpu.make_async_copy(img_in, img.at[pl.ds(0, ROWS)], load_sem.at[1])
    load_cap.start()
    load_img.start()

    barrier = pltpu.get_barrier_semaphore()
    for m in members_a:
        pl.semaphore_signal(barrier, inc=1, device_id=group_a(*m), device_id_type=MESH)
    for m in members_b:
        pl.semaphore_signal(barrier, inc=1, device_id=group_b(*m), device_id_type=MESH)

    lane = lax.broadcasted_iota(jnp.int32, (1, 128), 1)
    low_half = lane < 64
    pos_lo = pos_in[0:1, 0:128]
    pos_hi = jnp.concatenate([pos_in[0:1, 128:192], jnp.zeros((1, 64), jnp.int32)], axis=1)
    ok_lo = valid_in[0:1, 0:128]
    ok_hi = jnp.concatenate([valid_in[0:1, 128:192], jnp.zeros((1, 64), jnp.int32)], axis=1)
    meta[0, 0:1, :] = pos_lo + pos_hi * 32768
    meta[0, 1:2, :] = ok_lo + ok_hi * 2

    row_match[...] = jnp.zeros_like(row_match)
    col_max[...] = jnp.full_like(col_max, 2 * LOW)
    col_sum[...] = jnp.zeros_like(col_sum)
    col_match[...] = jnp.zeros_like(col_match)
    part[...] = jnp.zeros_like(part)

    pl.semaphore_wait(barrier, len(members_a) + len(members_b))

    meta_copies = {}
    for d, s, o in members_a:
        there = place_a((4 - d) % 4, s, o)
        meta_copies[(d, s, o)] = copy(
            meta.at[0], meta.at[there], meta_send.at[place_a(d, s, o)], meta_recv.at[there], group_a(d, s, o)
        )
        meta_copies[(d, s, o)].start()

    ring_a = (group_a(1, 0, 0), group_a(3, 0, 0), group_a(0, 1, 0))
    ring_b = (group_b(1, 0), group_b(3, 0), group_b(0, 1))
    other = group_a(0, 0, 1)

    def cap_copy(link, r):
        src, dst = row_place(sent(link, r), 0), row_place(3 * (r + 1) + link, 0)
        return copy(
            cap.at[pl.ds(src, PIECE)], cap.at[pl.ds(dst, PIECE)],
            cap_send.at[link * ROUNDS + r], cap_recv.at[link * ROUNDS + r], ring_a[link],
        )

    def img_copy(link, r):
        src, dst = sent(link, r) * PIECE, (3 * (r + 1) + link) * PIECE
        return copy(
            img.at[pl.ds(src, PIECE)], img.at[pl.ds(dst, PIECE)],
            img_send.at[link * ROUNDS + r], img_recv.at[link * ROUNDS + r], ring_b[link],
        )

    def core_copy(slot):
        return copy(
            cap.at[pl.ds(row_place(slot, 0), PIECE)], cap.at[pl.ds(row_place(slot, 1), PIECE)],
            core_send.at[slot], core_recv.at[slot], other,
        )

    def forward(after, which=(0, 1)):
        for r in range(ROUNDS):
            for link in range(3):
                if release(link, r) == after:
                    if 0 in which:
                        cap_copy(link, r).start()
                    if 1 in which:
                        img_copy(link, r).start()

    def arrive(r):
        for link in range(3):
            cap_copy(link, r - 1).wait_recv()
            core_copy(3 * r + link).start()
        for link in range(3):
            img_copy(link, r - 1).wait_recv()
        forward(r)

    def arrive_core(r):
        for link in range(3):
            core_copy(3 * r + link).wait_recv()

    load_cap.wait()
    load_img.wait()
    for r in range(2):
        for link in range(3):
            cap_copy(link, r).start()
            img_copy(link, r).start()
    for t in range(3):
        core_copy(t).start()

    for d, s, o in members_a:
        meta_copies[(d, s, o)].wait_recv()

    word = jnp.zeros((1, 128), jnp.int32)
    for d in range(4):
        for s in range(2):
            for o in range(2):
                at = lax.rem(x + d, 4) * 4 + lax.rem(c + o, 2) * 2 + lax.rem(yl + s, 2)
                word = word | lax.shift_left(
                    meta[place_a(d, s, o), 1:2, :], jnp.broadcast_to(2 * at, (1, 128))
                )
    mine = yh * 4 + z
    table[mine] = word
    table_copies = {}
    for d, s in members_b:
        table_copies[(d, s)] = copy(
            table.at[mine], table.at[mine], table_send.at[place_b(d, s)],
            table_recv.at[place_b((4 - d) % 4, s)], group_b(d, s),
        )
        table_copies[(d, s)].start()
    for link in range(3):
        cap_copy(link, 2).start()
        img_copy(link, 2).start()

    arrive(1)

    for d, s in members_b:
        there = lax.rem(yh + s, 2) * 4 + lax.rem(z + d, 4)
        copy(
            table.at[there], table.at[there], table_send.at[place_b(d, s)],
            table_recv.at[place_b(d, s)], group_b(d, s),
        ).wait_recv()

    for pair in range(12):
        ids, flags = [], []
        for half in range(2):
            slot = 2 * pair + half
            d, s, t = next(k for k, v in SLOT.items() if v == slot)
            ph, pz, pc = lax.rem(yh + s, 2), lax.rem(z + d, 4), lax.rem(yl + s, 2)
            device = (((x * 2 + ph) * 4 + pz) * 2 + c) * 2 + pc
            shift = 2 * (x * 4 + c * 2 + pc) + (1 if t == 2 else 0)
            bits = lax.shift_right_logical(table[ph * 4 + pz], jnp.broadcast_to(shift, (1, 128))) & 1
            if (t == 1) != (half == 1):
                bits = pltpu.roll(bits, 64, 1)
            flags.append(bits)
            ids.append(device * ROWS + t * PIECE - half * 64 + lane)
        flag = jnp.where(low_half, flags[0], flags[1])
        col_bias[0:1, pair * 128 : (pair + 1) * 128] = jnp.where(flag > 0, 0.0, LOW)
        col_id[0:1, pair * 128 : (pair + 1) * 128] = jnp.where(low_half, ids[0], ids[1]).astype(jnp.float32)

    words = jnp.concatenate([table[b] for b in range(8)], axis=0)
    bytes_ = jnp.concatenate(
        [(lax.shift_right_logical(words, jnp.full((8, 128), 8 * q, jnp.int32)) & 255) for q in range(4)], axis=0
    ).astype(jnp.float32).astype(jnp.bfloat16)
    sub = lax.broadcasted_iota(jnp.int32, (128, 128), 0)
    sub8 = lax.broadcasted_iota(jnp.int32, (8, 128), 0)

    def look_up(p):
        pick = ((p >> 6) * 171) >> 9
        row = p - pick * ROWS
        high = (row >= 128).astype(jnp.int32)
        at = row - 128 * high
        here = (((pick >> 4) & 1) << 2) + ((pick >> 2) & 3)
        bit = ((((pick >> 5) << 2) + (pick & 3)) << 1) + high
        hot = (sub == at).astype(jnp.float32).astype(jnp.bfloat16)
        got = jnp.dot(bytes_, hot, preferred_element_type=jnp.float32).astype(jnp.int32)
        value = jnp.zeros((1, 128), jnp.int32)
        for q in range(4):
            mine_q = jnp.sum(jnp.where(sub8 == here, got[8 * q : 8 * q + 8], 0), axis=0, keepdims=True)
            value = jnp.where((bit >> 3) == q, mine_q, value)
        return lax.shift_right_logical(value, bit & 7) & 1

    for d in range(4):
        for s in range(2):
            for o in range(2):
                packed = meta[place_a(d, s, o), 0:1, :]
                for half in range(2):
                    p = (packed & 32767) if half == 0 else (packed >> 15)
                    ok = look_up(p)
                    if (d, s, o) == (0, 0, 0):
                        own_ok[half : half + 1, :] = ok.astype(jnp.float32)
                    wanted = jnp.where(ok > 0, p, -1).astype(jnp.float32)
                    turned = jnp.transpose(jnp.broadcast_to(wanted, (128, 128)))
                    if half == 0:
                        key[pl.ds(row_place(SLOT[(d, s, 0)], o), PIECE)] = turned[:64]
                        key[pl.ds(row_place(SLOT[(d, s, 1)], o), PIECE)] = turned[64:]
                    else:
                        key[pl.ds(row_place(SLOT[(d, s, 2)], o), PIECE)] = turned[:64]

    for t in range(3):
        core_copy(t).wait_recv()
    arrive_core(1)

    scores = (score0, score1)

    def multiply(i, into):
        tile, block = place(i)
        rows = pl.ds(pl.multiple_of(tile * TILE, TILE), TILE)
        cols = pl.ds(pl.multiple_of(block * BLOCK, BLOCK), BLOCK)
        into[...] = lax.dot_general(
            cap[rows, :], img[cols, :], (((1,), (1,)), ((), ())), preferred_element_type=jnp.float32
        )

    def statistics(i, held):
        tile, block = place(i)
        first = pl.multiple_of(tile * TILE, TILE)
        cols = [pl.ds(pl.multiple_of(block * BLOCK, BLOCK) + 128 * h, 128) for h in range(2)]
        bias = [jnp.broadcast_to(col_bias[0:1, cols[h]], (PIECE, 128)) for h in range(2)]
        ids = [jnp.broadcast_to(col_id[0:1, cols[h]], (PIECE, 128)) for h in range(2)]
        before = [col_max[:, cols[h]] for h in range(2)]
        peak = list(before)
        for k in range(TILE // PIECE):
            rows = pl.ds(first + k * PIECE, PIECE)
            here = pl.ds(k * PIECE, PIECE)
            row_bias = jnp.where(key[rows, :] < 0, LOW, 0.0)
            values = []
            for h in range(2):
                u = held[here, 128 * h : 128 * h + 128] * LOG2E + bias[h] + row_bias
                held[here, 128 * h : 128 * h + 128] = u
                peak[h] = jnp.maximum(peak[h], jnp.max(u.reshape(PIECE // 8, 8, 128), axis=0))
                values.append(u)
            high = jnp.max(jnp.maximum(values[0], values[1]), axis=1, keepdims=True)
            row_max[block, rows, :] = jnp.broadcast_to(high, (PIECE, 128))
        total = [jnp.zeros((8, 128), jnp.float32) for _ in range(2)]
        match = [col_match[:, cols[h]] for h in range(2)]
        for k in range(TILE // PIECE):
            rows = pl.ds(first + k * PIECE, PIECE)
            here = pl.ds(k * PIECE, PIECE)
            high = row_max[block, rows, :]
            wanted = key[rows, :]
            found = row_match[rows, :]
            row_total = None
            for h in range(2):
                u = held[here, 128 * h : 128 * h + 128]
                e = jnp.exp2(u - high)
                row_total = e if row_total is None else row_total + e
                hit = wanted == ids[h]
                found = jnp.where(hit, u, found)
                for g in range(PIECE // 8):
                    part_u = u[8 * g : 8 * g + 8]
                    total[h] = total[h] + jnp.exp2(part_u - peak[h])
                    match[h] = jnp.where(hit[8 * g : 8 * g + 8], part_u, match[h])
            row_sum[block, rows, :] = row_total
            row_match[rows, :] = found
        for h in range(2):
            col_sum[:, cols[h]] = col_sum[:, cols[h]] * jnp.exp2(before[h] - peak[h]) + total[h]
            col_max[:, cols[h]] = peak[h]
            col_match[:, cols[h]] = match[h]

    multiply(jnp.int32(0), scores[0])

    @pl.loop(0, ITEMS // 2)
    def _(step):
        for half in range(2):
            i = step * 2 + half
            nxt = jnp.minimum(i + 1, ITEMS - 1)
            for r in range(2, ROUNDS + 1):
                if (STARTS[r] - 1) % 2 == half:
                    @pl.when(i + 1 == STARTS[r])
                    def _():
                        arrive(r)
                if (PAIRS_AT[r] - 1) % 2 == half:
                    @pl.when(i + 1 == PAIRS_AT[r])
                    def _():
                        arrive_core(r)
            multiply(nxt, scores[1 - half])
            statistics(i, scores[half])

    sub64 = lax.broadcasted_iota(jnp.int32, (PIECE, 128), 0)
    lane64 = lax.broadcasted_iota(jnp.int32, (PIECE, 128), 1)

    def row_result(slot, core, shift):
        rows = pl.ds(row_place(slot, core), PIECE)
        high = row_max[0, rows, :]
        for b in range(1, BLOCKS):
            high = jnp.maximum(high, row_max[b, rows, :])
        total = None
        for b in range(BLOCKS):
            term = row_sum[b, rows, :] * jnp.exp2(row_max[b, rows, :] - high)
            total = term if total is None else total + term
        lse = high + jnp.log2(jnp.sum(total, axis=1, keepdims=True))
        found = jnp.sum(row_match[rows, :], axis=1, keepdims=True)
        mine_lane = lane64 == sub64 + shift
        return (
            jnp.sum(jnp.where(mine_lane, lse, 0.0), axis=0, keepdims=True),
            jnp.sum(jnp.where(mine_lane, found, 0.0), axis=0, keepdims=True),
        )

    row_copies = []
    for d in range(4):
        for s in range(2):
            for o in range(2):
                at = place_a(d, s, o)
                first, second, third = (
                    row_result(SLOT[(d, s, t)], o, 64 if t == 1 else 0) for t in range(3)
                )
                into = row_got if at == 0 else row_msg
                into[at, 0:1, :] = first[0] + second[0]
                into[at, 1:2, :] = third[0]
                into[at, 2:3, :] = first[1] + second[1]
                into[at, 3:4, :] = third[1]
                if at:
                    there = place_a((4 - d) % 4, s, o)
                    out = copy(
                        row_msg.at[at], row_got.at[there], row_send.at[at], row_recv.at[there], group_a(d, s, o)
                    )
                    out.start()
                    row_copies.append(out)

    def merged(peak, total):
        high = jnp.max(peak, axis=0, keepdims=True)
        return high + jnp.log2(jnp.sum(total * jnp.exp2(peak - high), axis=0, keepdims=True))

    columns = []
    for pair in range(12):
        cols = pl.ds(pair * 128, 128)
        columns.append((
            merged(col_max[:, cols], col_sum[:, cols]),
            jnp.sum(col_match[:, cols], axis=0, keepdims=True),
        ))

    def third_of(slot, which, right):
        value = columns[slot // 2][which]
        return pltpu.roll(value, 64, 1) if (slot % 2 == 1) != right else value

    col_copies = []
    for d in range(4):
        for s in range(2):
            at = place_b(d, s)
            into = col_got if at == 0 else col_msg
            for which in range(2):
                left = third_of(SLOT[(d, s, 0)], which, False)
                right = third_of(SLOT[(d, s, 1)], which, True)
                into[at, 2 * which : 2 * which + 1, :] = jnp.where(low_half, left, right)
                into[at, 2 * which + 1 : 2 * which + 2, :] = third_of(SLOT[(d, s, 2)], which, False)
            if at:
                there = place_b((4 - d) % 4, s)
                out = copy(
                    col_msg.at[at], col_got.at[there], col_send.at[at], col_recv.at[there], group_b(d, s)
                )
                out.start()
                col_copies.append(out)

    for out in row_copies + col_copies:
        out.wait_recv()

    def joined(got):
        values = got[:, 0:2, :]
        high = jnp.max(values, axis=0)
        total = jnp.sum(jnp.exp2(values - high[None]), axis=0)
        return (high + jnp.log2(total) - jnp.sum(got[:, 2:4, :], axis=0)) * LN2

    usable = (lax.broadcasted_iota(jnp.int32, (2, 128), 0) == 0) | (
        lax.broadcasted_iota(jnp.int32, (2, 128), 1) < 64
    )
    cap_loss = jnp.where((own_ok[0:2, :] > 0) & usable, joined(row_got), 0.0)
    own_flags = jnp.concatenate([ok_lo, ok_hi], axis=0)
    img_loss = jnp.where((own_flags > 0) & usable, joined(col_got), 0.0)
    cap_out[0:1, 0:128] = cap_loss[0:1]
    cap_out[0:1, 128:192] = cap_loss[1:2, 0:64]
    img_out[0:1, 0:128] = img_loss[0:1]
    img_out[0:1, 128:192] = img_loss[1:2, 0:64]

    def spread(value, here, got, send, recv, members, index, target):
        here[0:1, :] = value
        outs = []
        for m in members:
            there = index((4 - m[0]) % 4, *m[1:])
            out = copy(here, got.at[there], send.at[index(*m)], recv.at[there], target(*m))
            out.start()
            outs.append(out)
        for out in outs:
            out.wait_recv()
        got[0] = here[...]
        return jnp.sum(got[...], axis=0)[0:1], outs

    both = cap_loss + img_loss
    total, outs_a = spread(
        both[0:1] + both[1:2], part, part_got, a_send, a_recv, members_a, place_a, group_a
    )
    part2[...] = jnp.zeros_like(part2)
    total, outs_b = spread(total, part2, part2_got, b_send, b_recv, members_b, place_b, group_b)
    count = jnp.zeros((8, 128), jnp.int32)
    for b in range(32):
        count = count + (lax.shift_right_logical(words, jnp.full((8, 128), b, jnp.int32)) & 1)
    real = jnp.sum(jnp.sum(count, axis=0, keepdims=True).astype(jnp.float32), axis=1, keepdims=True)
    loss_out[0:1, :] = jnp.broadcast_to(
        jnp.sum(total, axis=1, keepdims=True) / (2.0 * real), (1, 128)
    )

    for r in range(ROUNDS):
        for link in range(3):
            cap_copy(link, r).wait_send()
            img_copy(link, r).wait_send()
    for slot in range(24):
        core_copy(slot).wait_send()
    for out in [*meta_copies.values(), *table_copies.values(), *row_copies, *col_copies, *outs_a, *outs_b]:
        out.wait_send()


def local(captions, images, positives, valid):
    f32, i32 = jnp.float32, jnp.int32
    dma = pltpu.SemaphoreType.DMA
    vmem = pl.BlockSpec(memory_space=pltpu.VMEM)
    hbm = pl.BlockSpec(memory_space=pl.ANY)
    cap_loss, img_loss, loss = pl.pallas_call(
        kernel,
        out_shape=(
            jax.ShapeDtypeStruct((1, ROWS), f32),
            jax.ShapeDtypeStruct((1, ROWS), f32),
            jax.ShapeDtypeStruct((1, 128), f32),
        ),
        in_specs=[hbm, hbm, vmem, vmem],
        out_specs=(vmem, vmem, vmem),
        scratch_shapes=[
            pltpu.VMEM((TILES * TILE, WIDTH), jnp.bfloat16),
            pltpu.VMEM((BLOCKS * BLOCK, WIDTH), jnp.bfloat16),
            pltpu.VMEM((TILE, BLOCK), f32),
            pltpu.VMEM((TILE, BLOCK), f32),
            pltpu.VMEM((TILES * TILE, 128), f32),
            pltpu.VMEM((BLOCKS, TILES * TILE, 128), f32),
            pltpu.VMEM((BLOCKS, TILES * TILE, 128), f32),
            pltpu.VMEM((TILES * TILE, 128), f32),
            pltpu.VMEM((8, BLOCKS * BLOCK), f32),
            pltpu.VMEM((8, BLOCKS * BLOCK), f32),
            pltpu.VMEM((8, BLOCKS * BLOCK), f32),
            pltpu.VMEM((1, BLOCKS * BLOCK), f32),
            pltpu.VMEM((1, BLOCKS * BLOCK), f32),
            pltpu.VMEM((16, 2, 128), i32),
            pltpu.VMEM((8, 1, 128), i32),
            pltpu.VMEM((2, 128), f32),
            pltpu.VMEM((16, 4, 128), f32),
            pltpu.VMEM((16, 4, 128), f32),
            pltpu.VMEM((8, 4, 128), f32),
            pltpu.VMEM((8, 4, 128), f32),
            pltpu.VMEM((8, 128), f32),
            pltpu.VMEM((16, 8, 128), f32),
            pltpu.VMEM((8, 128), f32),
            pltpu.VMEM((8, 8, 128), f32),
            dma((2,)),
            dma((21,)), dma((21,)), dma((21,)), dma((21,)), dma((24,)), dma((24,)),
            dma((16,)), dma((16,)), dma((8,)), dma((8,)),
            dma((16,)), dma((16,)), dma((8,)), dma((8,)),
            dma((16,)), dma((16,)), dma((8,)), dma((8,)),
        ],
        compiler_params=pltpu.CompilerParams(
            collective_id=0, has_side_effects=True, vmem_limit_bytes=62 * 1024 * 1024
        ),
    )(captions, images, positives.reshape(1, ROWS), valid.reshape(1, ROWS))
    return cap_loss.reshape(ROWS), img_loss.reshape(ROWS), loss[0, 0]


def solution(mesh):
    torus = Mesh(mesh.devices.reshape(4, 2, 4, 2, mesh.shape["rep"]), AXES)
    return jax.shard_map(
        local,
        mesh=torus,
        in_specs=(P(AXES, None), P(AXES, None), P(AXES), P(AXES)),
        out_specs=(P(AXES), P(AXES), P()),
        check_vma=False,
    )
```

time: 403 us -> 71.6 us (0.18)
  waiting for transfers between devices: 169 us -> 0 us
  local copies, waits for them, and re-layouts: 77.3 us -> 1.86 us
  blocking collectives: 72.7 us -> 0 us
  Pallas kernels: 0 us -> 67.7 us
  other arithmetic: 27 us -> 0 us
  starting transfers between devices: 19.3 us -> 0 us
  between operations: 19.6 us -> 1.82 us
  matrix products: 17.6 us -> 0 us
    unnamed x3 -> x0, waiting for transfers between devices: 160 us -> none
    gather x2 -> x0, local copies, waits for them, and re-layouts: 69.5 us -> none  [the longest x1 68 us: local(): piece_ok = jnp.take(image_flags, all_targets, axis=0)]
    pallas_call x0 -> x1, Pallas kernels: none -> 67.7 us  [local(): pl.pallas_call(kernel, out_shape=(jax.ShapeDtypeStruct((1, ROWS), f32), j...]
    all_gather x4 -> x0, blocking collectives: 38.5 us -> none  [all_in_one(): both, at, found = (lax.all_gather(jnp.concatenate(lines), axis), 0, {})]
    psum x5 -> x0, blocking collectives: 34.2 us -> none  [by_axis(): return functools.reduce(lax.psum, axes, shard)]
    all_to_all x3 -> x0, starting transfers between devices: 19.2 us -> none  [sent_to_all(): lax.all_to_all(jnp.broadcast_to(shard[None], (count, *shard.shape)), axis...]
    dot_general x1 -> x0, matrix products: 17.6 us -> none  [local(): lax.dot_general(piece, image_block, (((1,), (1,)), ((), ())), preferred_e...]
    reduce_sum x3 -> x0, other arithmetic: 12.9 us -> none  [the longest x1 10.8 us: fold_columns(): column_match = jnp.sum(jnp.where(is_positive, scores, 0.0), axis=0)]
  transfers between devices with their start and end apart: 5 -> 0, of which waited for: 2 -> 0; matrix products, arithmetic and copies ran while one was open for 19% -> 0% of each run, Pallas kernels for 0% -> 0%
where the time goes in v1:
time: 71.6 us; the launch traced here: 71.4 us
  Pallas kernels  67.7 us (95%)
  local copies, waits for them, and re-layouts  1.86 us (3%)
  between operations  1.82 us (3%)
    pallas_call x1, Pallas kernels, local(): pl.pallas_call(kernel, out_shape=(jax.ShapeDtypeStruct((1, ROWS), f32), j...  67.7 us
    unnamed x8, local copies, waits for them, and re-layouts  1.86 us

profile of v1, /device:TPU:1, one launch (start us, length us, event | category | flops | bytes accessed | tf_op | source)
XLA Modules:
  0.0 71.4 jit_solution(3203982821010239037)
XLA Ops:
  0.6 67.7 %shard_map.67 = (f32[1,192]{1,0:T(1,128)}, f32[1,192]{1,0:T(1,128)}, f32[1,128]{1,0:T(1,128)}) custom-call(bf16[192,768]{1,0:T(8,128)(2,1)} %cap_in.1, bf16[192,768]{1,0:T(8,128)(2,1)} %img_in.1, s32[1,192]{1,0:T(1,128)} %bitcast.6, s32[1,192]{1,0:T(1,128)} %bitcast.7), custom_call_target="tpu_custom_call" | custom-call | tf_op jit(solution)/shard_map/pallas_call | solution.py:528
  68.4 0.0 copy-start.1
  68.4 0.6 copy-done.1
  69.0 0.0 copy-start
  69.0 0.6 copy.10
  69.6 0.1 copy-done
  69.6 0.0 copy-start.2
  69.6 0.6 copy.11
  70.2 0.0 copy-done.2
Async XLA Ops:
  68.4 0.6 copy-start.1
  69.0 0.6 copy-start
  69.6 0.6 copy-start.2

commit v2 on v1

--- a/solution.py
+++ b/solution.py
@@ -64,6 +64,10 @@
 
 ORDER, STARTS, PAIRS_AT = items()
 ITEMS = len(ORDER)
+STEPS = ITEMS // 2
+EARLY = 2
+AT_STEP = {r: max(STARTS[r] // 2, 1) for r in STARTS}
+CORE_AT_STEP = {r: max(PAIRS_AT[r] // 2, 1) for r in STARTS}
 
 
 def segments():
@@ -101,7 +105,7 @@
 def kernel(
     cap_in, img_in, pos_in, valid_in,
     cap_out, img_out, loss_out,
-    cap, img, score0, score1, key, row_max, row_sum, row_match,
+    cap, img, score0, score1, score2, score3, key, row_bias, row_max, row_sum, row_match,
     col_max, col_sum, col_match, col_bias, col_id,
     meta, table, own_ok, row_msg, row_got, col_msg, col_got, part, part_got, part2, part2_got,
     load_sem, cap_send, cap_recv, img_send, img_recv, core_send, core_recv,
@@ -109,6 +113,7 @@
     a_send, a_recv, b_send, b_recv,
 ):
     x, yh, z, c, yl = (lax.axis_index(a) for a in AXES)
+    scores = (score0, score1, score2, score3)
 
     def group_a(d, s, o):
         return (lax.rem(x + d, 4), yh, z, lax.rem(c + o, 2), lax.rem(yl + s, 2))
@@ -151,9 +156,6 @@
     meta[0, 1:2, :] = ok_lo + ok_hi * 2
 
     row_match[...] = jnp.zeros_like(row_match)
-    col_max[...] = jnp.full_like(col_max, 2 * LOW)
-    col_sum[...] = jnp.zeros_like(col_sum)
-    col_match[...] = jnp.zeros_like(col_match)
     part[...] = jnp.zeros_like(part)
 
     pl.semaphore_wait(barrier, len(members_a) + len(members_b))
@@ -213,10 +215,11 @@
 
     load_cap.wait()
     load_img.wait()
-    for r in range(2):
+    for r in range(3):
         for link in range(3):
             cap_copy(link, r).start()
-            img_copy(link, r).start()
+            if r == 0:
+                img_copy(link, r).start()
     for t in range(3):
         core_copy(t).start()
 
@@ -240,11 +243,12 @@
             table_recv.at[place_b((4 - d) % 4, s)], group_b(d, s),
         )
         table_copies[(d, s)].start()
-    for link in range(3):
-        cap_copy(link, 2).start()
-        img_copy(link, 2).start()
-
-    arrive(1)
+    for r in range(1, 3):
+        for link in range(3):
+            img_copy(link, r).start()
+
+    for r in range(1, EARLY + 1):
+        arrive(r)
 
     for d, s in members_b:
         there = lax.rem(yh + s, 2) * 4 + lax.rem(z + d, 4)
@@ -303,17 +307,16 @@
                         own_ok[half : half + 1, :] = ok.astype(jnp.float32)
                     wanted = jnp.where(ok > 0, p, -1).astype(jnp.float32)
                     turned = jnp.transpose(jnp.broadcast_to(wanted, (128, 128)))
-                    if half == 0:
-                        key[pl.ds(row_place(SLOT[(d, s, 0)], o), PIECE)] = turned[:64]
-                        key[pl.ds(row_place(SLOT[(d, s, 1)], o), PIECE)] = turned[64:]
-                    else:
-                        key[pl.ds(row_place(SLOT[(d, s, 2)], o), PIECE)] = turned[:64]
+                    for t in (0, 1) if half == 0 else (2,):
+                        rows = pl.ds(row_place(SLOT[(d, s, t)], o), PIECE)
+                        value = turned[64 * (t % 2) : 64 * (t % 2) + 64]
+                        key[rows, :] = value
+                        row_bias[rows, :] = jnp.where(value < 0, LOW, 0.0)
 
     for t in range(3):
         core_copy(t).wait_recv()
-    arrive_core(1)
-
-    scores = (score0, score1)
+    for r in range(1, EARLY + 1):
+        arrive_core(r)
 
     def multiply(i, into):
         tile, block = place(i)
@@ -323,28 +326,34 @@
             cap[rows, :], img[cols, :], (((1,), (1,)), ((), ())), preferred_element_type=jnp.float32
         )
 
-    def statistics(i, held):
+    def peaks(i, held):
         tile, block = place(i)
         first = pl.multiple_of(tile * TILE, TILE)
         cols = [pl.ds(pl.multiple_of(block * BLOCK, BLOCK) + 128 * h, 128) for h in range(2)]
         bias = [jnp.broadcast_to(col_bias[0:1, cols[h]], (PIECE, 128)) for h in range(2)]
-        ids = [jnp.broadcast_to(col_id[0:1, cols[h]], (PIECE, 128)) for h in range(2)]
-        before = [col_max[:, cols[h]] for h in range(2)]
-        peak = list(before)
+        peak = [None, None]
         for k in range(TILE // PIECE):
             rows = pl.ds(first + k * PIECE, PIECE)
             here = pl.ds(k * PIECE, PIECE)
-            row_bias = jnp.where(key[rows, :] < 0, LOW, 0.0)
+            low = row_bias[rows, :]
             values = []
             for h in range(2):
-                u = held[here, 128 * h : 128 * h + 128] * LOG2E + bias[h] + row_bias
+                u = held[here, 128 * h : 128 * h + 128] * LOG2E + bias[h] + low
                 held[here, 128 * h : 128 * h + 128] = u
-                peak[h] = jnp.maximum(peak[h], jnp.max(u.reshape(PIECE // 8, 8, 128), axis=0))
+                top = jnp.max(u.reshape(PIECE // 8, 8, 128), axis=0)
+                peak[h] = top if peak[h] is None else jnp.maximum(peak[h], top)
                 values.append(u)
             high = jnp.max(jnp.maximum(values[0], values[1]), axis=1, keepdims=True)
             row_max[block, rows, :] = jnp.broadcast_to(high, (PIECE, 128))
+        return peak
+
+    def sums(i, held, peak):
+        tile, block = place(i)
+        first = pl.multiple_of(tile * TILE, TILE)
+        cols = [pl.ds(pl.multiple_of(block * BLOCK, BLOCK) + 128 * h, 128) for h in range(2)]
+        ids = [jnp.broadcast_to(col_id[0:1, cols[h]], (PIECE, 128)) for h in range(2)]
         total = [jnp.zeros((8, 128), jnp.float32) for _ in range(2)]
-        match = [col_match[:, cols[h]] for h in range(2)]
+        match = [jnp.zeros((8, 128), jnp.float32) for _ in range(2)]
         for k in range(TILE // PIECE):
             rows = pl.ds(first + k * PIECE, PIECE)
             here = pl.ds(k * PIECE, PIECE)
@@ -365,28 +374,35 @@
             row_sum[block, rows, :] = row_total
             row_match[rows, :] = found
         for h in range(2):
-            col_sum[:, cols[h]] = col_sum[:, cols[h]] * jnp.exp2(before[h] - peak[h]) + total[h]
-            col_max[:, cols[h]] = peak[h]
-            col_match[:, cols[h]] = match[h]
+            col_max[tile, :, cols[h]] = peak[h]
+            col_sum[tile, :, cols[h]] = total[h]
+            col_match[tile, :, cols[h]] = match[h]
 
     multiply(jnp.int32(0), scores[0])
-
-    @pl.loop(0, ITEMS // 2)
-    def _(step):
+    multiply(jnp.int32(1), scores[1])
+
+    @pl.loop(0, STEPS // 2)
+    def _(turn):
         for half in range(2):
-            i = step * 2 + half
-            nxt = jnp.minimum(i + 1, ITEMS - 1)
-            for r in range(2, ROUNDS + 1):
-                if (STARTS[r] - 1) % 2 == half:
-                    @pl.when(i + 1 == STARTS[r])
+            step = turn * 2 + half
+            for r in range(EARLY + 1, ROUNDS + 1):
+                if (AT_STEP[r] - 1) % 2 == half:
+                    @pl.when(step + 1 == AT_STEP[r])
                     def _():
                         arrive(r)
-                if (PAIRS_AT[r] - 1) % 2 == half:
-                    @pl.when(i + 1 == PAIRS_AT[r])
+                if (CORE_AT_STEP[r] - 1) % 2 == half:
+                    @pl.when(step + 1 == CORE_AT_STEP[r])
                     def _():
                         arrive_core(r)
-            multiply(nxt, scores[1 - half])
-            statistics(i, scores[half])
+            i = 2 * step
+            nxt = jnp.minimum(i + 2, ITEMS - 2)
+            now = scores[2 * half : 2 * half + 2]
+            later = scores[2 - 2 * half : 4 - 2 * half]
+            multiply(nxt, later[0])
+            multiply(nxt + 1, later[1])
+            tops = [peaks(i + k, now[k]) for k in range(2)]
+            for k in range(2):
+                sums(i + k, now[k], tops[k])
 
     sub64 = lax.broadcasted_iota(jnp.int32, (PIECE, 128), 0)
     lane64 = lax.broadcasted_iota(jnp.int32, (PIECE, 128), 1)
@@ -430,15 +446,16 @@
                     row_copies.append(out)
 
     def merged(peak, total):
-        high = jnp.max(peak, axis=0, keepdims=True)
-        return high + jnp.log2(jnp.sum(total * jnp.exp2(peak - high), axis=0, keepdims=True))
+        high = jnp.max(jnp.max(peak, axis=0), axis=0, keepdims=True)
+        total = jnp.sum(total * jnp.exp2(peak - high[None]), axis=0)
+        return high + jnp.log2(jnp.sum(total, axis=0, keepdims=True))
 
     columns = []
     for pair in range(12):
         cols = pl.ds(pair * 128, 128)
         columns.append((
-            merged(col_max[:, cols], col_sum[:, cols]),
-            jnp.sum(col_match[:, cols], axis=0, keepdims=True),
+            merged(col_max[:, :, cols], col_sum[:, :, cols]),
+            jnp.sum(jnp.sum(col_match[:, :, cols], axis=0), axis=0, keepdims=True),
         ))
 
     def third_of(slot, which, right):
@@ -537,15 +554,15 @@
         scratch_shapes=[
             pltpu.VMEM((TILES * TILE, WIDTH), jnp.bfloat16),
             pltpu.VMEM((BLOCKS * BLOCK, WIDTH), jnp.bfloat16),
-            pltpu.VMEM((TILE, BLOCK), f32),
-            pltpu.VMEM((TILE, BLOCK), f32),
+            *[pltpu.VMEM((TILE, BLOCK), f32)] * 4,
+            pltpu.VMEM((TILES * TILE, 128), f32),
             pltpu.VMEM((TILES * TILE, 128), f32),
             pltpu.VMEM((BLOCKS, TILES * TILE, 128), f32),
             pltpu.VMEM((BLOCKS, TILES * TILE, 128), f32),
             pltpu.VMEM((TILES * TILE, 128), f32),
-            pltpu.VMEM((8, BLOCKS * BLOCK), f32),
-            pltpu.VMEM((8, BLOCKS * BLOCK), f32),
-            pltpu.VMEM((8, BLOCKS * BLOCK), f32),
+            pltpu.VMEM((TILES, 8, BLOCKS * BLOCK), f32),
+            pltpu.VMEM((TILES, 8, BLOCKS * BLOCK), f32),
+            pltpu.VMEM((TILES, 8, BLOCKS * BLOCK), f32),
             pltpu.VMEM((1, BLOCKS * BLOCK), f32),
             pltpu.VMEM((1, BLOCKS * BLOCK), f32),
             pltpu.VMEM((16, 2, 128), i32),

time: 71.6 us -> 60.2 us (0.84)
  Pallas kernels: 67.7 us -> 56.3 us
    pallas_call x1, Pallas kernels: 67.7 us -> 56.3 us  [local(): pl.pallas_call(kernel, out_shape=(jax.ShapeDtypeStruct((1, ROWS), f32), j...]
where the time goes in v2:
time: 60.2 us; the launch traced here: 60 us
  Pallas kernels  56.3 us (94%)
  local copies, waits for them, and re-layouts  1.86 us (3%)
  between operations  1.82 us (3%)
    pallas_call x1, Pallas kernels, local(): pl.pallas_call(kernel, out_shape=(jax.ShapeDtypeStruct((1, ROWS), f32), j...  56.3 us
    unnamed x8, local copies, waits for them, and re-layouts  1.86 us

profile of v2, /device:TPU:1, one launch (start us, length us, event | category | flops | bytes accessed | tf_op | source)
XLA Modules:
  0.0 60.0 jit_solution(5237737340514406629)
XLA Ops:
  0.6 56.3 %shard_map.67 = (f32[1,192]{1,0:T(1,128)}, f32[1,192]{1,0:T(1,128)}, f32[1,128]{1,0:T(1,128)}) custom-call(bf16[192,768]{1,0:T(8,128)(2,1)} %cap_in.1, bf16[192,768]{1,0:T(8,128)(2,1)} %img_in.1, s32[1,192]{1,0:T(1,128)} %bitcast.6, s32[1,192]{1,0:T(1,128)} %bitcast.7), custom_call_target="tpu_custom_call" | custom-call | tf_op jit(solution)/shard_map/pallas_call | solution.py:545
  56.9 0.0 copy-start.1
  57.0 0.6 %copy-done.1 = f32[1,192]{1,0:T(1,128)S(1)} copy-done((f32[1,192]{1,0:T(1,128)S(1)}, f32[1,192]{1,0:T(1,128)}, u32[]{:S(2)}) %copy-start.1) | copy-done | bytes 792
  57.6 0.0 copy-start
  57.6 0.6 copy.10
  58.1 0.1 copy-done
  58.2 0.0 copy-start.2
  58.2 0.6 copy.11
  58.8 0.0 copy-done.2
Async XLA Ops:
  56.9 0.6 %copy-start.1 = (f32[1,192]{1,0:T(1,128)S(1)}, f32[1,192]{1,0:T(1,128)}, u32[]{:S(2)}) copy-start(f32[1,192]{1,0:T(1,128)} %get-tuple-element.6) | copy-start | bytes 2308
  57.6 0.6 %copy-start = (f32[1,192]{1,0:T(1,128)S(1)}, f32[1,192]{1,0:T(1,128)}, u32[]{:S(2)}) copy-start(f32[1,192]{1,0:T(1,128)} %get-tuple-element.7) | copy-start | bytes 2308
  58.2 0.6 copy-start.2

commit v3 on v2

--- a/solution.py
+++ b/solution.py
@@ -31,6 +31,9 @@
 for _link, _list in enumerate(ARRIVALS):
     for _r, _chunk in enumerate(_list):
         SLOT[_chunk] = 3 * (_r + 1) + _link
+
+
+RIGHT = {k for (_, _, t), k in SLOT.items() if t == 1}
 
 
 def sent(link, r):
@@ -66,7 +69,7 @@
 ITEMS = len(ORDER)
 STEPS = ITEMS // 2
 EARLY = 2
-AT_STEP = {r: max(STARTS[r] // 2, 1) for r in STARTS}
+AT_STEP = {3: 1, 4: 4, 5: 7, 6: 11, 7: 16}
 CORE_AT_STEP = {r: max(PAIRS_AT[r] // 2, 1) for r in STARTS}
 
 
@@ -107,9 +110,11 @@
     cap_out, img_out, loss_out,
     cap, img, score0, score1, score2, score3, key, row_bias, row_max, row_sum, row_match,
     col_max, col_sum, col_match, col_bias, col_id,
-    meta, table, own_ok, row_msg, row_got, col_msg, col_got, part, part_got, part2, part2_got,
+    meta, table, cap_ok, img_ok, row_all, row_msg, row_got, row_lse, col_all, col_msg, col_got, col_lse,
+    part_a, part_b,
     load_sem, cap_send, cap_recv, img_send, img_recv, core_send, core_recv,
     meta_send, meta_recv, table_send, table_recv, row_send, row_recv, col_send, col_recv,
+    all_send, all_recv, call_send, call_recv,
     a_send, a_recv, b_send, b_recv,
 ):
     x, yh, z, c, yl = (lax.axis_index(a) for a in AXES)
@@ -156,7 +161,6 @@
     meta[0, 1:2, :] = ok_lo + ok_hi * 2
 
     row_match[...] = jnp.zeros_like(row_match)
-    part[...] = jnp.zeros_like(part)
 
     pl.semaphore_wait(barrier, len(members_a) + len(members_b))
 
@@ -218,7 +222,7 @@
     for r in range(3):
         for link in range(3):
             cap_copy(link, r).start()
-            if r == 0:
+            if r < 2:
                 img_copy(link, r).start()
     for t in range(3):
         core_copy(t).start()
@@ -243,9 +247,8 @@
             table_recv.at[place_b((4 - d) % 4, s)], group_b(d, s),
         )
         table_copies[(d, s)].start()
-    for r in range(1, 3):
-        for link in range(3):
-            img_copy(link, r).start()
+    for link in range(3):
+        img_copy(link, 2).start()
 
     for r in range(1, EARLY + 1):
         arrive(r)
@@ -256,6 +259,15 @@
             table.at[there], table.at[there], table_send.at[place_b(d, s)],
             table_recv.at[place_b(d, s)], group_b(d, s),
         ).wait_recv()
+
+    for d in range(4):
+        for s in range(2):
+            ph, pz, pc = lax.rem(yh + s, 2), lax.rem(z + d, 4), lax.rem(yl + s, 2)
+            base = (pz * 2 + pc) * 2
+            for half in range(2):
+                shift = 2 * (x * 4 + c * 2 + pc) + half
+                bits = lax.shift_right_logical(table[ph * 4 + pz], jnp.broadcast_to(shift, (1, 128))) & 1
+                img_ok[pl.ds(base + half, 1), :] = bits.astype(jnp.float32)
 
     for pair in range(12):
         ids, flags = [], []
@@ -298,13 +310,22 @@
 
     for d in range(4):
         for s in range(2):
+            base = (lax.rem(x + d, 4) * 2 + lax.rem(yl + s, 2)) * 3
+            last = jnp.zeros((1, 128), jnp.float32)
             for o in range(2):
                 packed = meta[place_a(d, s, o), 0:1, :]
+                core = lax.rem(c + o, 2)
                 for half in range(2):
                     p = (packed & 32767) if half == 0 else (packed >> 15)
                     ok = look_up(p)
-                    if (d, s, o) == (0, 0, 0):
-                        own_ok[half : half + 1, :] = ok.astype(jnp.float32)
+                    real = ok.astype(jnp.float32)
+                    if half == 0:
+                        cap_ok[pl.ds(base + core, 1), :] = real
+                    else:
+                        real = jnp.where(low_half, real, 0.0)
+                        last = last + jnp.where(core == 1, pltpu.roll(real, 64, 1), real)
+                        if o == 1:
+                            cap_ok[pl.ds(base + 2, 1), :] = last
                     wanted = jnp.where(ok > 0, p, -1).astype(jnp.float32)
                     turned = jnp.transpose(jnp.broadcast_to(wanted, (128, 128)))
                     for t in (0, 1) if half == 0 else (2,):
@@ -418,32 +439,33 @@
             total = term if total is None else total + term
         lse = high + jnp.log2(jnp.sum(total, axis=1, keepdims=True))
         found = jnp.sum(row_match[rows, :], axis=1, keepdims=True)
-        mine_lane = lane64 == sub64 + shift
+        lse_lane = lane64 == sub64 + shift
+        lane_shift = 64 if slot in RIGHT else 0
+        found_lane = lane64 == sub64 + lane_shift
         return (
-            jnp.sum(jnp.where(mine_lane, lse, 0.0), axis=0, keepdims=True),
-            jnp.sum(jnp.where(mine_lane, found, 0.0), axis=0, keepdims=True),
-        )
-
-    row_copies = []
+            jnp.sum(jnp.where(lse_lane, lse, 0.0), axis=0, keepdims=True),
+            jnp.sum(jnp.where(found_lane, found, 0.0), axis=0, keepdims=True),
+        )
+
+    matched = jnp.zeros((1, 128), jnp.float32)
     for d in range(4):
         for s in range(2):
+            base = (lax.rem(x + d, 4) * 2 + lax.rem(yl + s, 2)) * 3
+            last = jnp.zeros((1, 128), jnp.float32)
             for o in range(2):
-                at = place_a(d, s, o)
-                first, second, third = (
-                    row_result(SLOT[(d, s, t)], o, 64 if t == 1 else 0) for t in range(3)
-                )
+                at, core = place_a(d, s, o), lax.rem(c + o, 2)
+                first, second = (row_result(SLOT[(d, s, t)], o, 64 * t) for t in range(2))
+                third = row_result(SLOT[(d, s, 2)], o, 64 * core)
+                row_all[0, pl.ds(base + core, 1), :] = first[0] + second[0]
+                last = last + third[0]
                 into = row_got if at == 0 else row_msg
-                into[at, 0:1, :] = first[0] + second[0]
-                into[at, 1:2, :] = third[0]
-                into[at, 2:3, :] = first[1] + second[1]
-                into[at, 3:4, :] = third[1]
-                if at:
-                    there = place_a((4 - d) % 4, s, o)
-                    out = copy(
-                        row_msg.at[at], row_got.at[there], row_send.at[at], row_recv.at[there], group_a(d, s, o)
-                    )
-                    out.start()
-                    row_copies.append(out)
+                into[at, 0:1, :] = first[1] + second[1]
+                into[at, 1:2, :] = third[1]
+                matched = matched + first[1] + second[1] + third[1]
+            row_all[0, pl.ds(base + 2, 1), :] = last
+    row_got[0, 2:3, :] = matched
+    for at in range(1, 16):
+        row_msg[at, 2:3, :] = matched
 
     def merged(peak, total):
         high = jnp.max(jnp.max(peak, axis=0), axis=0, keepdims=True)
@@ -462,69 +484,85 @@
         value = columns[slot // 2][which]
         return pltpu.roll(value, 64, 1) if (slot % 2 == 1) != right else value
 
-    col_copies = []
     for d in range(4):
         for s in range(2):
             at = place_b(d, s)
+            base = (lax.rem(z + d, 4) * 2 + lax.rem(yl + s, 2)) * 2
             into = col_got if at == 0 else col_msg
             for which in range(2):
                 left = third_of(SLOT[(d, s, 0)], which, False)
                 right = third_of(SLOT[(d, s, 1)], which, True)
-                into[at, 2 * which : 2 * which + 1, :] = jnp.where(low_half, left, right)
-                into[at, 2 * which + 1 : 2 * which + 2, :] = third_of(SLOT[(d, s, 2)], which, False)
-            if at:
-                there = place_b((4 - d) % 4, s)
-                out = copy(
-                    col_msg.at[at], col_got.at[there], col_send.at[at], col_recv.at[there], group_b(d, s)
-                )
-                out.start()
-                col_copies.append(out)
-
-    for out in row_copies + col_copies:
-        out.wait_recv()
-
-    def joined(got):
-        values = got[:, 0:2, :]
-        high = jnp.max(values, axis=0)
-        total = jnp.sum(jnp.exp2(values - high[None]), axis=0)
-        return (high + jnp.log2(total) - jnp.sum(got[:, 2:4, :], axis=0)) * LN2
-
-    usable = (lax.broadcasted_iota(jnp.int32, (2, 128), 0) == 0) | (
-        lax.broadcasted_iota(jnp.int32, (2, 128), 1) < 64
-    )
-    cap_loss = jnp.where((own_ok[0:2, :] > 0) & usable, joined(row_got), 0.0)
-    own_flags = jnp.concatenate([ok_lo, ok_hi], axis=0)
-    img_loss = jnp.where((own_flags > 0) & usable, joined(col_got), 0.0)
-    cap_out[0:1, 0:128] = cap_loss[0:1]
-    cap_out[0:1, 128:192] = cap_loss[1:2, 0:64]
-    img_out[0:1, 0:128] = img_loss[0:1]
-    img_out[0:1, 128:192] = img_loss[1:2, 0:64]
-
-    def spread(value, here, got, send, recv, members, index, target):
-        here[0:1, :] = value
+                both = jnp.where(low_half, left, right)
+                last = third_of(SLOT[(d, s, 2)], which, False)
+                if which == 0:
+                    col_all[0, pl.ds(base, 1), :] = both
+                    col_all[0, pl.ds(base + 1, 1), :] = last
+                else:
+                    into[at, 0:1, :] = both
+                    into[at, 1:2, :] = last
+
+    def exchange(members, index, target, pairs):
         outs = []
         for m in members:
-            there = index((4 - m[0]) % 4, *m[1:])
-            out = copy(here, got.at[there], send.at[index(*m)], recv.at[there], target(*m))
-            out.start()
-            outs.append(out)
-        for out in outs:
-            out.wait_recv()
-        got[0] = here[...]
-        return jnp.sum(got[...], axis=0)[0:1], outs
-
-    both = cap_loss + img_loss
-    total, outs_a = spread(
-        both[0:1] + both[1:2], part, part_got, a_send, a_recv, members_a, place_a, group_a
-    )
-    part2[...] = jnp.zeros_like(part2)
-    total, outs_b = spread(total, part2, part2_got, b_send, b_recv, members_b, place_b, group_b)
+            here, there = index(*m), index((4 - m[0]) % 4, *m[1:])
+            for src, dst, send, recv in pairs:
+                outs.append(copy(
+                    src(here), dst.at[there], send.at[here], recv.at[there], target(*m)
+                ))
+                outs[-1].start()
+        return outs
+
+    outs = exchange(members_a, place_a, group_a, [
+        (lambda here: row_all.at[0], row_all, all_send, all_recv),
+        (lambda here: row_msg.at[here], row_got, row_send, row_recv),
+    ])
+    outs += exchange(members_b, place_b, group_b, [
+        (lambda here: col_all.at[0], col_all, call_send, call_recv),
+        (lambda here: col_msg.at[here], col_got, col_send, col_recv),
+    ])
+    for out in outs:
+        out.wait_recv()
+
+    def joined(values):
+        high = jnp.max(values, axis=0)
+        return high + jnp.log2(jnp.sum(jnp.exp2(values - high[None]), axis=0))
+
+    row_lse[...] = joined(row_all[...])
+    col_lse[...] = joined(col_all[...])
+    row_part = jnp.sum(jnp.where(cap_ok[...] > 0, row_lse[...], 0.0), axis=0, keepdims=True)
+    found = jnp.sum(row_got[...], axis=0)
+    part_b[0] = row_part - 2.0 * found[2:3]
+    odd = lax.broadcasted_iota(jnp.int32, (16, 128), 0) & 1
+    wide = lax.broadcasted_iota(jnp.int32, (16, 128), 1)
+    counted = (img_ok[...] > 0) & ((odd == 0) | (wide < 64))
+    part_a[0] = jnp.sum(jnp.where(counted, col_lse[...], 0.0), axis=0, keepdims=True)
+    outs2 = exchange(members_a, place_a, group_a, [(lambda here: part_a.at[0], part_a, a_send, a_recv)])
+    outs2 += exchange(members_b, place_b, group_b, [(lambda here: part_b.at[0], part_b, b_send, b_recv)])
+
+    base = (x * 2 + yl) * 3
+    cap_lo = row_lse[pl.ds(base + c, 1), :] - found[0:1]
+    cap_hi = row_lse[pl.ds(base + 2, 1), :]
+    cap_hi = jnp.where(c == 1, pltpu.roll(cap_hi, 64, 1), cap_hi) - found[1:2]
+    real_hi = cap_ok[pl.ds(base + 2, 1), :]
+    real_hi = jnp.where(c == 1, pltpu.roll(real_hi, 64, 1), real_hi)
+    cap_out[0:1, 0:128] = jnp.where(cap_ok[pl.ds(base + c, 1), :] > 0, cap_lo * LN2, 0.0)
+    cap_out[0:1, 128:192] = jnp.where(real_hi > 0, cap_hi * LN2, 0.0)[:, 0:64]
+    base = (z * 2 + yl) * 2
+    found = jnp.sum(col_got[...], axis=0)
+    img_lo = col_lse[pl.ds(base, 1), :] - found[0:1]
+    img_hi = col_lse[pl.ds(base + 1, 1), :] - found[1:2]
+    img_out[0:1, 0:128] = jnp.where(ok_lo > 0, img_lo * LN2, 0.0)
+    img_out[0:1, 128:192] = jnp.where(ok_hi > 0, img_hi * LN2, 0.0)[:, 0:64]
     count = jnp.zeros((8, 128), jnp.int32)
     for b in range(32):
         count = count + (lax.shift_right_logical(words, jnp.full((8, 128), b, jnp.int32)) & 1)
     real = jnp.sum(jnp.sum(count, axis=0, keepdims=True).astype(jnp.float32), axis=1, keepdims=True)
+
+    for out in outs2:
+        out.wait_recv()
+    total = jnp.sum(part_a[...], axis=0) + jnp.sum(part_b[...], axis=0)
     loss_out[0:1, :] = jnp.broadcast_to(
-        jnp.sum(total, axis=1, keepdims=True) / (2.0 * real), (1, 128)
+        jnp.sum(total, axis=1, keepdims=True) * LN2 / (2.0 * real), (1, 128)
     )
 
     for r in range(ROUNDS):
@@ -533,7 +571,7 @@
             img_copy(link, r).wait_send()
     for slot in range(24):
         core_copy(slot).wait_send()
-    for out in [*meta_copies.values(), *table_copies.values(), *row_copies, *col_copies, *outs_a, *outs_b]:
+    for out in [*meta_copies.values(), *table_copies.values(), *outs, *outs2]:
         out.wait_send()
 
 
@@ -567,17 +605,21 @@
             pltpu.VMEM((1, BLOCKS * BLOCK), f32),
             pltpu.VMEM((16, 2, 128), i32),
             pltpu.VMEM((8, 1, 128), i32),
-            pltpu.VMEM((2, 128), f32),
-            pltpu.VMEM((16, 4, 128), f32),
-            pltpu.VMEM((16, 4, 128), f32),
-            pltpu.VMEM((8, 4, 128), f32),
-            pltpu.VMEM((8, 4, 128), f32),
-            pltpu.VMEM((8, 128), f32),
-            pltpu.VMEM((16, 8, 128), f32),
-            pltpu.VMEM((8, 128), f32),
-            pltpu.VMEM((8, 8, 128), f32),
+            pltpu.VMEM((24, 128), f32),
+            pltpu.VMEM((16, 128), f32),
+            pltpu.VMEM((16, 24, 128), f32),
+            pltpu.VMEM((16, 3, 128), f32),
+            pltpu.VMEM((16, 3, 128), f32),
+            pltpu.VMEM((24, 128), f32),
+            pltpu.VMEM((8, 16, 128), f32),
+            pltpu.VMEM((8, 2, 128), f32),
+            pltpu.VMEM((8, 2, 128), f32),
+            pltpu.VMEM((16, 128), f32),
+            pltpu.VMEM((16, 1, 128), f32),
+            pltpu.VMEM((8, 1, 128), f32),
             dma((2,)),
             dma((21,)), dma((21,)), dma((21,)), dma((21,)), dma((24,)), dma((24,)),
+            dma((16,)), dma((16,)), dma((8,)), dma((8,)),
             dma((16,)), dma((16,)), dma((8,)), dma((8,)),
             dma((16,)), dma((16,)), dma((8,)), dma((8,)),
             dma((16,)), dma((16,)), dma((8,)), dma((8,)),

time: 60.2 us -> 54.8 us (0.910)
  Pallas kernels: 56.3 us -> 51 us
    pallas_call x1, Pallas kernels: 56.3 us -> 51 us  [local(): pl.pallas_call(kernel, out_shape=(jax.ShapeDtypeStruct((1, ROWS), f32), j...]
where the time goes in v3:
time: 54.8 us; the launch traced here: 54.6 us
  Pallas kernels  51 us (93%)
  local copies, waits for them, and re-layouts  1.86 us (3%)
  between operations  1.82 us (3%)
    pallas_call x1, Pallas kernels, local(): pl.pallas_call(kernel, out_shape=(jax.ShapeDtypeStruct((1, ROWS), f32), j...  51 us
    unnamed x8, local copies, waits for them, and re-layouts  1.86 us

profile of v3, /device:TPU:1, one launch (start us, length us, event | category | flops | bytes accessed | tf_op | source)
XLA Modules:
  0.0 54.6 jit_solution(4812943133404554685)
XLA Ops:
  0.6 51.0 %shard_map.67 = (f32[1,192]{1,0:T(1,128)}, f32[1,192]{1,0:T(1,128)}, f32[1,128]{1,0:T(1,128)}) custom-call(bf16[192,768]{1,0:T(8,128)(2,1)} %cap_in.1, bf16[192,768]{1,0:T(8,128)(2,1)} %img_in.1, s32[1,192]{1,0:T(1,128)} %bitcast.6, s32[1,192]{1,0:T(1,128)} %bitcast.7), custom_call_target="tpu_custom_call" | custom-call | tf_op jit(solution)/shard_map/pallas_call | solution.py:583
  51.6 0.0 copy-start.1
  51.6 0.6 %copy-done.1 = f32[1,192]{1,0:T(1,128)S(1)} copy-done((f32[1,192]{1,0:T(1,128)S(1)}, f32[1,192]{1,0:T(1,128)}, u32[]{:S(2)}) %copy-start.1) | copy-done | bytes 792
  52.2 0.0 copy-start
  52.2 0.6 %copy.10 = f32[192]{0:T(256)} copy(f32[192]{0:T(256)S(1)} %bitcast.9) | data formatting | bytes 1536
  52.8 0.1 copy-done
  52.9 0.0 copy-start.2
  52.9 0.6 %copy.11 = f32[192]{0:T(256)} copy(f32[192]{0:T(256)S(1)} %bitcast.8) | data formatting | bytes 1536
  53.4 0.0 copy-done.2
Async XLA Ops:
  51.6 0.6 %copy-start.1 = (f32[1,192]{1,0:T(1,128)S(1)}, f32[1,192]{1,0:T(1,128)}, u32[]{:S(2)}) copy-start(f32[1,192]{1,0:T(1,128)} %get-tuple-element.6) | copy-start | bytes 2308
  52.2 0.6 %copy-start = (f32[1,192]{1,0:T(1,128)S(1)}, f32[1,192]{1,0:T(1,128)}, u32[]{:S(2)}) copy-start(f32[1,192]{1,0:T(1,128)} %get-tuple-element.7) | copy-start | bytes 2308
  52.9 0.6 %copy-start.2 = (f32[1,128]{1,0:T(1,128)S(1)}, f32[1,128]{1,0:T(1,128)}, u32[]{:S(2)}) copy-start(f32[1,128]{1,0:T(1,128)} %get-tuple-element.8) | copy-start | bytes 1540

commit v4 on v3

--- a/solution.py
+++ b/solution.py
@@ -111,11 +111,8 @@
     cap, img, score0, score1, score2, score3, key, row_bias, row_max, row_sum, row_match,
     col_max, col_sum, col_match, col_bias, col_id,
     meta, table, cap_ok, img_ok, row_all, row_msg, row_got, row_lse, col_all, col_msg, col_got, col_lse,
-    part_a, part_b,
-    load_sem, cap_send, cap_recv, img_send, img_recv, core_send, core_recv,
-    meta_send, meta_recv, table_send, table_recv, row_send, row_recv, col_send, col_recv,
-    all_send, all_recv, call_send, call_recv,
-    a_send, a_recv, b_send, b_recv,
+    part_a, part_b, cap_res, img_res,
+    load_sem, out_sem, bulk_send, cap_recv, img_recv, core_recv, small_send, small_recv,
 ):
     x, yh, z, c, yl = (lax.axis_index(a) for a in AXES)
     scores = (score0, score1, score2, score3)
@@ -164,13 +161,9 @@
 
     pl.semaphore_wait(barrier, len(members_a) + len(members_b))
 
-    meta_copies = {}
     for d, s, o in members_a:
         there = place_a((4 - d) % 4, s, o)
-        meta_copies[(d, s, o)] = copy(
-            meta.at[0], meta.at[there], meta_send.at[place_a(d, s, o)], meta_recv.at[there], group_a(d, s, o)
-        )
-        meta_copies[(d, s, o)].start()
+        copy(meta.at[0], meta.at[there], small_send.at[0], small_recv.at[0], group_a(d, s, o)).start()
 
     ring_a = (group_a(1, 0, 0), group_a(3, 0, 0), group_a(0, 1, 0))
     ring_b = (group_b(1, 0), group_b(3, 0), group_b(0, 1))
@@ -180,21 +173,25 @@
         src, dst = row_place(sent(link, r), 0), row_place(3 * (r + 1) + link, 0)
         return copy(
             cap.at[pl.ds(src, PIECE)], cap.at[pl.ds(dst, PIECE)],
-            cap_send.at[link * ROUNDS + r], cap_recv.at[link * ROUNDS + r], ring_a[link],
+            bulk_send.at[0], cap_recv.at[r], ring_a[link],
         )
 
     def img_copy(link, r):
         src, dst = sent(link, r) * PIECE, (3 * (r + 1) + link) * PIECE
         return copy(
             img.at[pl.ds(src, PIECE)], img.at[pl.ds(dst, PIECE)],
-            img_send.at[link * ROUNDS + r], img_recv.at[link * ROUNDS + r], ring_b[link],
+            bulk_send.at[1], img_recv.at[r], ring_b[link],
         )
 
-    def core_copy(slot):
+    def core_copy(r):
         return copy(
-            cap.at[pl.ds(row_place(slot, 0), PIECE)], cap.at[pl.ds(row_place(slot, 1), PIECE)],
-            core_send.at[slot], core_recv.at[slot], other,
+            cap.at[pl.ds(r * TILE, ROWS)], cap.at[pl.ds(r * TILE + ROWS, ROWS)],
+            bulk_send.at[2], core_recv.at[r], other,
         )
+
+    def all_of(ref, count, send, recv):
+        part = ref.at[pl.ds(0, count)]
+        return copy(part, part, send, recv, other)
 
     def forward(after, which=(0, 1)):
         for r in range(ROUNDS):
@@ -206,16 +203,13 @@
                         img_copy(link, r).start()
 
     def arrive(r):
-        for link in range(3):
-            cap_copy(link, r - 1).wait_recv()
-            core_copy(3 * r + link).start()
-        for link in range(3):
-            img_copy(link, r - 1).wait_recv()
+        all_of(cap, ROWS, bulk_send.at[0], cap_recv.at[r - 1]).wait_recv()
+        core_copy(r).start()
+        all_of(img, ROWS, bulk_send.at[1], img_recv.at[r - 1]).wait_recv()
         forward(r)
 
     def arrive_core(r):
-        for link in range(3):
-            core_copy(3 * r + link).wait_recv()
+        core_copy(r).wait_recv()
 
     load_cap.wait()
     load_img.wait()
@@ -224,11 +218,9 @@
             cap_copy(link, r).start()
             if r < 2:
                 img_copy(link, r).start()
-    for t in range(3):
-        core_copy(t).start()
-
-    for d, s, o in members_a:
-        meta_copies[(d, s, o)].wait_recv()
+    core_copy(0).start()
+
+    all_of(meta, 15, small_send.at[0], small_recv.at[0]).wait_recv()
 
     word = jnp.zeros((1, 128), jnp.int32)
     for d in range(4):
@@ -240,25 +232,15 @@
                 )
     mine = yh * 4 + z
     table[mine] = word
-    table_copies = {}
     for d, s in members_b:
-        table_copies[(d, s)] = copy(
-            table.at[mine], table.at[mine], table_send.at[place_b(d, s)],
-            table_recv.at[place_b((4 - d) % 4, s)], group_b(d, s),
-        )
-        table_copies[(d, s)].start()
+        copy(table.at[mine], table.at[mine], small_send.at[1], small_recv.at[1], group_b(d, s)).start()
     for link in range(3):
         img_copy(link, 2).start()
 
     for r in range(1, EARLY + 1):
         arrive(r)
 
-    for d, s in members_b:
-        there = lax.rem(yh + s, 2) * 4 + lax.rem(z + d, 4)
-        copy(
-            table.at[there], table.at[there], table_send.at[place_b(d, s)],
-            table_recv.at[place_b(d, s)], group_b(d, s),
-        ).wait_recv()
+    all_of(table, 7, small_send.at[1], small_recv.at[1]).wait_recv()
 
     for d in range(4):
         for s in range(2):
@@ -334,9 +316,7 @@
                         key[rows, :] = value
                         row_bias[rows, :] = jnp.where(value < 0, LOW, 0.0)
 
-    for t in range(3):
-        core_copy(t).wait_recv()
-    for r in range(1, EARLY + 1):
+    for r in range(EARLY + 1):
         arrive_core(r)
 
     def multiply(i, into):
@@ -502,24 +482,21 @@
                     into[at, 1:2, :] = last
 
     def exchange(members, index, target, pairs):
-        outs = []
         for m in members:
             here, there = index(*m), index((4 - m[0]) % 4, *m[1:])
-            for src, dst, send, recv in pairs:
-                outs.append(copy(
-                    src(here), dst.at[there], send.at[here], recv.at[there], target(*m)
-                ))
-                outs[-1].start()
-        return outs
-
-    outs = exchange(members_a, place_a, group_a, [
-        (lambda here: row_all.at[0], row_all, all_send, all_recv),
-        (lambda here: row_msg.at[here], row_got, row_send, row_recv),
+            for src, dst, k in pairs:
+                copy(src(here), dst.at[there], small_send.at[k], small_recv.at[k], target(*m)).start()
+
+    def exchanged(refs):
+        return [all_of(ref, count, small_send.at[k], small_recv.at[k]) for ref, count, k in refs]
+
+    exchange(members_a, place_a, group_a, [
+        (lambda here: row_all.at[0], row_all, 2), (lambda here: row_msg.at[here], row_got, 3),
     ])
-    outs += exchange(members_b, place_b, group_b, [
-        (lambda here: col_all.at[0], col_all, call_send, call_recv),
-        (lambda here: col_msg.at[here], col_got, col_send, col_recv),
+    exchange(members_b, place_b, group_b, [
+        (lambda here: col_all.at[0], col_all, 4), (lambda here: col_msg.at[here], col_got, 5),
     ])
+    outs = exchanged([(row_all, 15, 2), (row_got, 15, 3), (col_all, 7, 4), (col_got, 7, 5)])
     for out in outs:
         out.wait_recv()
 
@@ -536,8 +513,9 @@
     wide = lax.broadcasted_iota(jnp.int32, (16, 128), 1)
     counted = (img_ok[...] > 0) & ((odd == 0) | (wide < 64))
     part_a[0] = jnp.sum(jnp.where(counted, col_lse[...], 0.0), axis=0, keepdims=True)
-    outs2 = exchange(members_a, place_a, group_a, [(lambda here: part_a.at[0], part_a, a_send, a_recv)])
-    outs2 += exchange(members_b, place_b, group_b, [(lambda here: part_b.at[0], part_b, b_send, b_recv)])
+    exchange(members_a, place_a, group_a, [(lambda here: part_a.at[0], part_a, 6)])
+    exchange(members_b, place_b, group_b, [(lambda here: part_b.at[0], part_b, 7)])
+    outs2 = exchanged([(part_a, 15, 6), (part_b, 7, 7)])
 
     base = (x * 2 + yl) * 3
     cap_lo = row_lse[pl.ds(base + c, 1), :] - found[0:1]
@@ -545,18 +523,31 @@
     cap_hi = jnp.where(c == 1, pltpu.roll(cap_hi, 64, 1), cap_hi) - found[1:2]
     real_hi = cap_ok[pl.ds(base + 2, 1), :]
     real_hi = jnp.where(c == 1, pltpu.roll(real_hi, 64, 1), real_hi)
-    cap_out[0:1, 0:128] = jnp.where(cap_ok[pl.ds(base + c, 1), :] > 0, cap_lo * LN2, 0.0)
-    cap_out[0:1, 128:192] = jnp.where(real_hi > 0, cap_hi * LN2, 0.0)[:, 0:64]
+    cap_res[0:128] = jnp.where(cap_ok[pl.ds(base + c, 1), :] > 0, cap_lo * LN2, 0.0).reshape(128)
+    cap_res[128:192] = jnp.where(real_hi > 0, cap_hi * LN2, 0.0)[:, 0:64].reshape(64)
     base = (z * 2 + yl) * 2
     found = jnp.sum(col_got[...], axis=0)
     img_lo = col_lse[pl.ds(base, 1), :] - found[0:1]
     img_hi = col_lse[pl.ds(base + 1, 1), :] - found[1:2]
-    img_out[0:1, 0:128] = jnp.where(ok_lo > 0, img_lo * LN2, 0.0)
-    img_out[0:1, 128:192] = jnp.where(ok_hi > 0, img_hi * LN2, 0.0)[:, 0:64]
+    img_res[0:128] = jnp.where(ok_lo > 0, img_lo * LN2, 0.0).reshape(128)
+    img_res[128:192] = jnp.where(ok_hi > 0, img_hi * LN2, 0.0)[:, 0:64].reshape(64)
+    results = [
+        pltpu.make_async_copy(cap_res, cap_out, out_sem.at[0]), pltpu.make_async_copy(img_res, img_out, out_sem.at[1])
+    ]
+    for result in results:
+        result.start()
     count = jnp.zeros((8, 128), jnp.int32)
     for b in range(32):
         count = count + (lax.shift_right_logical(words, jnp.full((8, 128), b, jnp.int32)) & 1)
     real = jnp.sum(jnp.sum(count, axis=0, keepdims=True).astype(jnp.float32), axis=1, keepdims=True)
+
+    all_of(cap, 3 * ROUNDS * PIECE, bulk_send.at[0], cap_recv.at[0]).wait_send()
+    all_of(img, 3 * ROUNDS * PIECE, bulk_send.at[1], img_recv.at[0]).wait_send()
+    all_of(cap, TILES * ROWS, bulk_send.at[2], core_recv.at[0]).wait_send()
+    for out in exchanged([(meta, 15, 0), (table, 7, 1)]) + outs:
+        out.wait_send()
+    for result in results:
+        result.wait()
 
     for out in outs2:
         out.wait_recv()
@@ -564,14 +555,7 @@
     loss_out[0:1, :] = jnp.broadcast_to(
         jnp.sum(total, axis=1, keepdims=True) * LN2 / (2.0 * real), (1, 128)
     )
-
-    for r in range(ROUNDS):
-        for link in range(3):
-            cap_copy(link, r).wait_send()
-            img_copy(link, r).wait_send()
-    for slot in range(24):
-        core_copy(slot).wait_send()
-    for out in [*meta_copies.values(), *table_copies.values(), *outs, *outs2]:
+    for out in outs2:
         out.wait_send()
 
 
@@ -583,12 +567,12 @@
     cap_loss, img_loss, loss = pl.pallas_call(
         kernel,
         out_shape=(
-            jax.ShapeDtypeStruct((1, ROWS), f32),
-            jax.ShapeDtypeStruct((1, ROWS), f32),
+            jax.ShapeDtypeStruct((ROWS,), f32),
+            jax.ShapeDtypeStruct((ROWS,), f32),
             jax.ShapeDtypeStruct((1, 128), f32),
         ),
         in_specs=[hbm, hbm, vmem, vmem],
-        out_specs=(vmem, vmem, vmem),
+        out_specs=(hbm, hbm, vmem),
         scratch_shapes=[
             pltpu.VMEM((TILES * TILE, WIDTH), jnp.bfloat16),
             pltpu.VMEM((BLOCKS * BLOCK, WIDTH), jnp.bfloat16),
@@ -617,18 +601,15 @@
             pltpu.VMEM((16, 128), f32),
             pltpu.VMEM((16, 1, 128), f32),
             pltpu.VMEM((8, 1, 128), f32),
-            dma((2,)),
-            dma((21,)), dma((21,)), dma((21,)), dma((21,)), dma((24,)), dma((24,)),
-            dma((16,)), dma((16,)), dma((8,)), dma((8,)),
-            dma((16,)), dma((16,)), dma((8,)), dma((8,)),
-            dma((16,)), dma((16,)), dma((8,)), dma((8,)),
-            dma((16,)), dma((16,)), dma((8,)), dma((8,)),
+            pltpu.VMEM((ROWS,), f32),
+            pltpu.VMEM((ROWS,), f32),
+            dma((2,)), dma((2,)), dma((3,)), dma((ROUNDS,)), dma((ROUNDS,)), dma((TILES,)), dma((8,)), dma((8,)),
         ],
         compiler_params=pltpu.CompilerParams(
             collective_id=0, has_side_effects=True, vmem_limit_bytes=62 * 1024 * 1024
         ),
     )(captions, images, positives.reshape(1, ROWS), valid.reshape(1, ROWS))
-    return cap_loss.reshape(ROWS), img_loss.reshape(ROWS), loss[0, 0]
+    return cap_loss, img_loss, loss[0, 0]
 
 
 def solution(mesh):

time: 54.8 us -> 51.3 us (0.936)
  Pallas kernels: 51 us -> 47.4 us
    pallas_call x1, Pallas kernels: 51 us -> 47.4 us  [local(): pl.pallas_call(kernel, out_shape=(jax.ShapeDtypeStruct((ROWS,), f32), jax...]
where the time goes in v4:
time: 51.3 us; the launch traced here: 51.1 us
  Pallas kernels  47.4 us (92%)
  local copies, waits for them, and re-layouts  1.86 us (4%)
  between operations  1.82 us (4%)
    pallas_call x1, Pallas kernels, local(): pl.pallas_call(kernel, out_shape=(jax.ShapeDtypeStruct((ROWS,), f32), jax...  47.4 us
    unnamed x8, local copies, waits for them, and re-layouts  1.86 us

profile of v4, /device:TPU:1, one launch (start us, length us, event | category | flops | bytes accessed | tf_op | source)
XLA Modules:
  0.0 51.1 jit_solution(17206626424814593545)
XLA Ops:
  0.6 47.4 %shard_map.67 = (f32[192]{0:T(256)}, f32[192]{0:T(256)}, f32[1,128]{1,0:T(1,128)}) custom-call(bf16[192,768]{1,0:T(8,128)(2,1)} %cap_in.1, bf16[192,768]{1,0:T(8,128)(2,1)} %img_in.1, s32[1,192]{1,0:T(1,128)} %bitcast.4, s32[1,192]{1,0:T(1,128)} %bitcast.5), custom_call_target="tpu_custom_call" | custom-call | tf_op jit(solution)/shard_map/pallas_call | solution.py:567
  48.1 0.0 copy-start.1
  48.1 0.6 %copy-done.1 = f32[192]{0:T(256)S(1)} copy-done((f32[192]{0:T(256)S(1)}, f32[192]{0:T(256)}, u32[]{:S(2)}) %copy-start.1) | copy-done | bytes 792
  48.7 0.0 copy-start
  48.7 0.6 %copy.10 = f32[192]{0:T(256)} copy(f32[192]{0:T(256)S(1)} %copy-done.1) | data formatting | bytes 1536
  49.3 0.1 copy-done
  49.4 0.0 copy-start.2
  49.4 0.6 %copy.11 = f32[192]{0:T(256)} copy(f32[192]{0:T(256)S(1)} %copy-done) | data formatting | bytes 1536
  49.9 0.0 copy-done.2
Async XLA Ops:
  48.1 0.6 %copy-start.1 = (f32[192]{0:T(256)S(1)}, f32[192]{0:T(256)}, u32[]{:S(2)}) copy-start(f32[192]{0:T(256)} %get-tuple-element.12) | copy-start | bytes 2308
  48.7 0.6 %copy-start = (f32[192]{0:T(256)S(1)}, f32[192]{0:T(256)}, u32[]{:S(2)}) copy-start(f32[192]{0:T(256)} %get-tuple-element.13) | copy-start | bytes 2308
  49.4 0.6 %copy-start.2 = (f32[1,128]{1,0:T(1,128)S(1)}, f32[1,128]{1,0:T(1,128)}, u32[]{:S(2)}) copy-start(f32[1,128]{1,0:T(1,128)} %get-tuple-element.8) | copy-start | bytes 1540

commit v5 on v4

--- a/solution.py
+++ b/solution.py
@@ -67,10 +67,11 @@
 
 ORDER, STARTS, PAIRS_AT = items()
 ITEMS = len(ORDER)
-STEPS = ITEMS // 2
+GROUP = 2
+STEPS = ITEMS // GROUP
 EARLY = 2
 AT_STEP = {3: 1, 4: 4, 5: 7, 6: 11, 7: 16}
-CORE_AT_STEP = {r: max(PAIRS_AT[r] // 2, 1) for r in STARTS}
+CORE_AT_STEP = {r: max(PAIRS_AT[r] // GROUP, 1) for r in STARTS}
 
 
 def segments():
@@ -125,6 +126,8 @@
 
     members_a = [(d, s, o) for d in range(4) for s in range(2) for o in range(2) if (d, s, o) != (0, 0, 0)]
     members_b = [(d, s) for d in range(4) for s in range(2) if (d, s) != (0, 0)]
+    members_a.sort(key=lambda m: -(2 * min(m[0], 4 - m[0]) + 2 * m[1] + m[2]))
+    members_b.sort(key=lambda m: -(min(m[0], 4 - m[0]) + m[1]))
 
     def copy(src, dst, ssem, rsem, target):
         return pltpu.make_async_remote_copy(
@@ -158,6 +161,8 @@
     meta[0, 1:2, :] = ok_lo + ok_hi * 2
 
     row_match[...] = jnp.zeros_like(row_match)
+    row_sum[...] = jnp.zeros_like(row_sum)
+    row_max[...] = jnp.full_like(row_max, 2 * LOW)
 
     pl.semaphore_wait(barrier, len(members_a) + len(members_b))
 
@@ -237,8 +242,20 @@
     for link in range(3):
         img_copy(link, 2).start()
 
+    def multiply(i, into):
+        tile, block = place(i)
+        rows = pl.ds(pl.multiple_of(tile * TILE, TILE), TILE)
+        cols = pl.ds(pl.multiple_of(block * BLOCK, BLOCK), BLOCK)
+        into[...] = lax.dot_general(
+            cap[rows, :], img[cols, :], (((1,), (1,)), ((), ())), preferred_element_type=jnp.float32
+        )
+
     for r in range(1, EARLY + 1):
         arrive(r)
+    arrive_core(0)
+    arrive_core(1)
+    for k in range(GROUP):
+        multiply(jnp.int32(k), scores[k])
 
     all_of(table, 7, small_send.at[1], small_recv.at[1]).wait_recv()
 
@@ -316,16 +333,7 @@
                         key[rows, :] = value
                         row_bias[rows, :] = jnp.where(value < 0, LOW, 0.0)
 
-    for r in range(EARLY + 1):
-        arrive_core(r)
-
-    def multiply(i, into):
-        tile, block = place(i)
-        rows = pl.ds(pl.multiple_of(tile * TILE, TILE), TILE)
-        cols = pl.ds(pl.multiple_of(block * BLOCK, BLOCK), BLOCK)
-        into[...] = lax.dot_general(
-            cap[rows, :], img[cols, :], (((1,), (1,)), ((), ())), preferred_element_type=jnp.float32
-        )
+    arrive_core(2)
 
     def peaks(i, held):
         tile, block = place(i)
@@ -344,8 +352,10 @@
                 top = jnp.max(u.reshape(PIECE // 8, 8, 128), axis=0)
                 peak[h] = top if peak[h] is None else jnp.maximum(peak[h], top)
                 values.append(u)
-            high = jnp.max(jnp.maximum(values[0], values[1]), axis=1, keepdims=True)
-            row_max[block, rows, :] = jnp.broadcast_to(high, (PIECE, 128))
+            old = row_max[rows, :]
+            high = jnp.maximum(jnp.max(jnp.maximum(values[0], values[1]), axis=1, keepdims=True), old)
+            row_sum[rows, :] = row_sum[rows, :] * jnp.exp2(old - high)
+            row_max[rows, :] = high
         return peak
 
     def sums(i, held, peak):
@@ -358,65 +368,63 @@
         for k in range(TILE // PIECE):
             rows = pl.ds(first + k * PIECE, PIECE)
             here = pl.ds(k * PIECE, PIECE)
-            high = row_max[block, rows, :]
+            high = row_max[rows, :]
             wanted = key[rows, :]
             found = row_match[rows, :]
-            row_total = None
+            row_total = row_sum[rows, :]
             for h in range(2):
                 u = held[here, 128 * h : 128 * h + 128]
                 e = jnp.exp2(u - high)
-                row_total = e if row_total is None else row_total + e
+                row_total = row_total + e
                 hit = wanted == ids[h]
                 found = jnp.where(hit, u, found)
                 for g in range(PIECE // 8):
                     part_u = u[8 * g : 8 * g + 8]
                     total[h] = total[h] + jnp.exp2(part_u - peak[h])
                     match[h] = jnp.where(hit[8 * g : 8 * g + 8], part_u, match[h])
-            row_sum[block, rows, :] = row_total
+            row_sum[rows, :] = row_total
             row_match[rows, :] = found
         for h in range(2):
             col_max[tile, :, cols[h]] = peak[h]
             col_sum[tile, :, cols[h]] = total[h]
             col_match[tile, :, cols[h]] = match[h]
 
-    multiply(jnp.int32(0), scores[0])
-    multiply(jnp.int32(1), scores[1])
-
-    @pl.loop(0, STEPS // 2)
+    def all_statistics(i, held):
+        for k in range(0, GROUP, 2):
+            tops = [peaks(i + k + j, held[k + j]) for j in range(2)]
+            for j in range(2):
+                sums(i + k + j, held[k + j], tops[j])
+
+    def advance(step, half):
+        for r in range(EARLY + 1, ROUNDS + 1):
+            if (AT_STEP[r] - 1) % 2 == half:
+                @pl.when(step + 1 == AT_STEP[r])
+                def _():
+                    arrive(r)
+            if (CORE_AT_STEP[r] - 1) % 2 == half:
+                @pl.when(step + 1 == CORE_AT_STEP[r])
+                def _():
+                    arrive_core(r)
+        i = GROUP * step
+        for k in range(GROUP):
+            multiply(i + GROUP + k, scores[(1 - half) * GROUP + k])
+        all_statistics(i, scores[half * GROUP :])
+
+    @pl.loop(0, (STEPS - 1) // 2)
     def _(turn):
         for half in range(2):
-            step = turn * 2 + half
-            for r in range(EARLY + 1, ROUNDS + 1):
-                if (AT_STEP[r] - 1) % 2 == half:
-                    @pl.when(step + 1 == AT_STEP[r])
-                    def _():
-                        arrive(r)
-                if (CORE_AT_STEP[r] - 1) % 2 == half:
-                    @pl.when(step + 1 == CORE_AT_STEP[r])
-                    def _():
-                        arrive_core(r)
-            i = 2 * step
-            nxt = jnp.minimum(i + 2, ITEMS - 2)
-            now = scores[2 * half : 2 * half + 2]
-            later = scores[2 - 2 * half : 4 - 2 * half]
-            multiply(nxt, later[0])
-            multiply(nxt + 1, later[1])
-            tops = [peaks(i + k, now[k]) for k in range(2)]
-            for k in range(2):
-                sums(i + k, now[k], tops[k])
+            advance(turn * 2 + half, half)
+
+    if STEPS % 2 == 0:
+        advance(jnp.int32(STEPS - 2), 0)
+    all_statistics(jnp.int32(ITEMS - GROUP), scores[((STEPS - 1) % 2) * GROUP :])
 
     sub64 = lax.broadcasted_iota(jnp.int32, (PIECE, 128), 0)
     lane64 = lax.broadcasted_iota(jnp.int32, (PIECE, 128), 1)
 
     def row_result(slot, core, shift):
         rows = pl.ds(row_place(slot, core), PIECE)
-        high = row_max[0, rows, :]
-        for b in range(1, BLOCKS):
-            high = jnp.maximum(high, row_max[b, rows, :])
-        total = None
-        for b in range(BLOCKS):
-            term = row_sum[b, rows, :] * jnp.exp2(row_max[b, rows, :] - high)
-            total = term if total is None else total + term
+        high, total = row_max[rows, :], row_sum[rows, :]
         lse = high + jnp.log2(jnp.sum(total, axis=1, keepdims=True))
         found = jnp.sum(row_match[rows, :], axis=1, keepdims=True)
         lse_lane = lane64 == sub64 + shift
@@ -579,8 +587,8 @@
             *[pltpu.VMEM((TILE, BLOCK), f32)] * 4,
             pltpu.VMEM((TILES * TILE, 128), f32),
             pltpu.VMEM((TILES * TILE, 128), f32),
-            pltpu.VMEM((BLOCKS, TILES * TILE, 128), f32),
-            pltpu.VMEM((BLOCKS, TILES * TILE, 128), f32),
+            pltpu.VMEM((TILES * TILE, 128), f32),
+            pltpu.VMEM((TILES * TILE, 128), f32),
             pltpu.VMEM((TILES * TILE, 128), f32),
             pltpu.VMEM((TILES, 8, BLOCKS * BLOCK), f32),
             pltpu.VMEM((TILES, 8, BLOCKS * BLOCK), f32),

time: 51.3 us -> 50.6 us (0.986)
  Pallas kernels: 47.4 us -> 46.5 us
    pallas_call x1, Pallas kernels: 47.4 us -> 46.5 us  [local(): pl.pallas_call(kernel, out_shape=(jax.ShapeDtypeStruct((ROWS,), f32), jax...]
where the time goes in v5:
time: 50.6 us; the launch traced here: 50.2 us
  Pallas kernels  46.5 us (92%)
  local copies, waits for them, and re-layouts  1.86 us (4%)
  between operations  1.82 us (4%)
    pallas_call x1, Pallas kernels, local(): pl.pallas_call(kernel, out_shape=(jax.ShapeDtypeStruct((ROWS,), f32), jax...  46.5 us
    unnamed x8, local copies, waits for them, and re-layouts  1.86 us

profile of v5, /device:TPU:1, one launch (start us, length us, event | category | flops | bytes accessed | tf_op | source)
XLA Modules:
  0.0 50.2 jit_solution(2048187130956156065)
XLA Ops:
  0.6 46.5 %shard_map.67 = (f32[192]{0:T(256)}, f32[192]{0:T(256)}, f32[1,128]{1,0:T(1,128)}) custom-call(bf16[192,768]{1,0:T(8,128)(2,1)} %cap_in.1, bf16[192,768]{1,0:T(8,128)(2,1)} %img_in.1, s32[1,192]{1,0:T(1,128)} %bitcast.4, s32[1,192]{1,0:T(1,128)} %bitcast.5), custom_call_target="tpu_custom_call" | custom-call | tf_op jit(solution)/shard_map/pallas_call | solution.py:575
  47.1 0.0 copy-start.1
  47.1 0.6 %copy-done.1 = f32[192]{0:T(256)S(1)} copy-done((f32[192]{0:T(256)S(1)}, f32[192]{0:T(256)}, u32[]{:S(2)}) %copy-start.1) | copy-done | bytes 792
  47.8 0.0 copy-start
  47.8 0.6 %copy.10 = f32[192]{0:T(256)} copy(f32[192]{0:T(256)S(1)} %copy-done.1) | data formatting | bytes 1536
  48.3 0.1 copy-done
  48.4 0.0 copy-start.2
  48.4 0.6 %copy.11 = f32[192]{0:T(256)} copy(f32[192]{0:T(256)S(1)} %copy-done) | data formatting | bytes 1536
  49.0 0.0 copy-done.2
Async XLA Ops:
  47.1 0.6 %copy-start.1 = (f32[192]{0:T(256)S(1)}, f32[192]{0:T(256)}, u32[]{:S(2)}) copy-start(f32[192]{0:T(256)} %get-tuple-element.12) | copy-start | bytes 2308
  47.8 0.6 %copy-start = (f32[192]{0:T(256)S(1)}, f32[192]{0:T(256)}, u32[]{:S(2)}) copy-start(f32[192]{0:T(256)} %get-tuple-element.13) | copy-start | bytes 2308
  48.4 0.6 %copy-start.2 = (f32[1,128]{1,0:T(1,128)S(1)}, f32[1,128]{1,0:T(1,128)}, u32[]{:S(2)}) copy-start(f32[1,128]{1,0:T(1,128)} %get-tuple-element.8) | copy-start | bytes 1540
